TPU v7x, 128 devices: a whole 4x4x4 slice. The times are simulated.
128 devices in a mesh: gx: 16 (over x, z), gy: 8 (over y, core).
Axes of the slice: x: 4, y: 4, z: 4, core: 2. Of those that a mesh axis runs over, the one named last changes fastest.
Arguments:
- base_state: float32 [4, 8, 1024, 1024], P(None, None, 'gx', 'gy'), may hold values from -6 to 6
- base_old: float32 [4, 8, 1024, 1024], P(None, None, 'gx', 'gy'), may hold values from -6 to 6
- fine_state: float32 [4, 8, 16, 264, 264], P(None, None, 'gx', 'gy'), may hold values from -6 to 6
- fine_old: float32 [4, 8, 16, 264, 264], P(None, None, 'gx', 'gy'), may hold values from -6 to 6
- coupling: float32 [4, 4], replicated, may hold values from -12 to 12
- patch_offsets: int32 [16, 2], replicated, may hold values from 1 to 935, as said below
- patch_group: int32 [16], replicated, may hold values from 0 to 15, each once
Outputs:
- base_residual: float32 [4, 8, 1024, 1024], P(None, None, 'gx', 'gy')
- fine_residual: float32 [4, 8, 16, 264, 264], P(None, None, 'gx', 'gy')
- residual_norm: float32 [], replicated
Inputs may be any that keep to these rules, and one draw needn't show every extreme that they name: `patch_offsets`: with the cycle of one base cell around it, each patch lies inside the grid, and no two patches or cycles share a cell. `patch_group`: every group owns exactly one patch.
All inputs are finite; a program needn't handle non-finite values.
Results may differ from a plain program's by a relative error of at most 0.0003.
Values sent between devices are 32-bit elements; how exact they have to be, the bound alone decides.
A program may use at most 128 MiB of HBM per device.

v0:
```python
import jax
import jax.numpy as jnp
from jax import lax
from jax.sharding import PartitionSpec as P

PC = 88
RATIO = 3


time_step = 0.1
viscosity = 0.2
vertical_mix = 0.5


def padded_2(block, sides, width):
    for axis, dim in sides:
        count = lax.axis_size(axis)
        forward = [(i, i + 1) for i in range(count - 1)]
        backward = [(target, source) for source, target in forward]
        low = lax.ppermute(
            lax.slice_in_dim(block, block.shape[dim] - width, None, axis=dim), axis, forward
        )
        high = lax.ppermute(lax.slice_in_dim(block, 0, width, axis=dim), axis, backward)
        block = jnp.concatenate([low, block, high], axis=dim)
    return block


def sent_together(arrays, axis, split_dim, concat_dim, along):
    both = jnp.concatenate(arrays, axis=along)
    result, at, done = (
        lax.all_to_all(both, axis, split_axis=split_dim, concat_axis=concat_dim, tiled=True),
        0,
        [],
    )
    for a in arrays:
        done.append(lax.slice_in_dim(result, at, at + a.shape[along], axis=along))
        at += a.shape[along]
    return tuple(done)


def in_order(blocks, dim):
    blocks = jnp.moveaxis(blocks, 0, dim)
    shape = blocks.shape
    return blocks.reshape(*shape[:dim], shape[dim] * shape[dim + 1], *shape[dim + 2 :])


def gather_packed(arrays, axis, dims):
    vector = jnp.concatenate([a.reshape(-1) for a in arrays])
    lines, at, done = (lax.all_gather(vector, axis), 0, [])
    for a, dim in zip(arrays, dims):
        blocks = lines[:, at : at + a.size].reshape(-1, *a.shape)
        done.append(in_order(blocks, dim))
        at += a.size
    return tuple(done)


def sent_to_all(value, axis):
    copies = jnp.broadcast_to(value, (lax.axis_size(axis), *value.shape))
    return lax.all_to_all(copies, axis, split_axis=0, concat_axis=0, tiled=True)


def gather_directly(value, axis, dim):
    return in_order(sent_to_all(value, axis), dim)


def tendency(padded, state, former, coupling, inverse):
    north = padded[:, :, 2:, 1:-1]
    south = padded[:, :, :-2, 1:-1]
    east = padded[:, :, 1:-1, 2:]
    west = padded[:, :, 1:-1, :-2]
    advect = (state[0:1] * (north - south) + state[1:2] * (east - west)) * (0.5 * inverse)
    laplace = (north + south + east + west - 4.0 * state) * (inverse * inverse)
    zero_level = jnp.zeros_like(state[:, :1])
    upper = jnp.concatenate([state[:, 1:], zero_level], axis=1)
    lower = jnp.concatenate([zero_level, state[:, :-1]], axis=1)
    vertical = 2.0 * state - upper - lower
    coupled = coupling[:, 0, None, None, None] * state[0:1]
    for source in range(1, state.shape[0]):
        coupled = coupled + coupling[:, source, None, None, None] * state[source : source + 1]
    return (
        state
        - former
        + time_step * (advect - viscosity * laplace + vertical_mix * vertical + coupled)
    )


def local(base_state, base_old, fine_state, fine_old, coupling, patch_offsets, patch_group):
    groups = lax.axis_size("gx")
    members = lax.axis_size("gy")
    row_block = lax.axis_index("gx")
    col_block = lax.axis_index("gy")
    fields, levels, block_x, block_y = base_state.shape
    grid_x = block_x * groups
    fine_rows = fine_state.shape[3]
    fine_cols = fine_state.shape[4]
    zero = jnp.zeros((), jnp.int32)
    padded = padded_2(base_state, (("gx", 2), ("gy", 3)), 1)
    base_tend = tendency(padded, base_state, base_old, coupling, 1.0)
    owner = (patch_group[None, :] == jnp.arange(groups, dtype=jnp.int32)[:, None]).astype(jnp.int32)
    placed = jnp.sum(owner[:, :, None] * patch_offsets[None, :, :], axis=1)
    mine = lax.dynamic_index_in_dim(placed, row_block, 0, keepdims=False)
    start_x = mine[0]
    start_y = mine[1]
    row_local = jnp.stack([placed[:, 0] - 1, placed[:, 0] + PC], axis=1) - row_block * block_x
    row_inside = ((row_local >= 0) & (row_local < block_x)).astype(jnp.float32)
    picked_rows = jnp.take(base_state, jnp.clip(row_local, 0, block_x - 1).reshape(-1), axis=2)
    row_slots = (
        picked_rows.reshape(fields, levels, groups, 2, block_y) * row_inside[None, None, :, :, None]
    )
    row_slots = jnp.moveaxis(row_slots, 2, 0)
    col_local = jnp.stack([placed[:, 1] - 1, placed[:, 1] + PC], axis=1) - col_block * block_y
    col_inside = ((col_local >= 0) & (col_local < block_y)).astype(jnp.float32)
    picked_cols = jnp.take(base_state, jnp.clip(col_local, 0, block_y - 1).reshape(-1), axis=3)
    col_slots = (
        picked_cols.reshape(fields, levels, block_x, groups, 2) * col_inside[None, None, None, :, :]
    )
    col_slots = jnp.transpose(col_slots, (3, 0, 1, 4, 2))
    received_rows, received_cols = sent_together((row_slots, col_slots), "gx", 0, 0, 4)
    rows_part = jnp.sum(received_rows, axis=0)
    cols_part = jnp.transpose(received_cols, (1, 2, 3, 0, 4)).reshape(fields, levels, 2, grid_x)
    cycle_rows, cycle_stack = gather_packed((rows_part, cols_part[None]), "gy", (3, 0))
    cycle_cols = jnp.sum(cycle_stack, axis=0)
    across_fine = start_y + jnp.arange(fine_cols, dtype=jnp.int32) // RATIO
    edges = jnp.take(cycle_rows, across_fine, axis=3)
    down_fine = start_x + (col_block * fine_rows + jnp.arange(fine_rows, dtype=jnp.int32)) // RATIO
    sides = jnp.take(cycle_cols, down_fine, axis=3)
    fine = fine_state[:, :, 0]
    former = fine_old[:, :, 0]
    halo_rows = padded_2(fine, (("gy", 2),), 1)
    first = jnp.where(col_block == 0, edges[:, :, 0:1], halo_rows[:, :, :1])
    last = jnp.where(col_block == members - 1, edges[:, :, 1:2], halo_rows[:, :, -1:])
    middle = jnp.concatenate([first, halo_rows[:, :, 1:-1], last], axis=2)
    corner = jnp.zeros((fields, levels, 1, 1), jnp.float32)
    left_col = jnp.concatenate([corner, sides[:, :, 0][..., None], corner], axis=2)
    right_col = jnp.concatenate([corner, sides[:, :, 1][..., None], corner], axis=2)
    padded_fine = jnp.concatenate([left_col, middle, right_col], axis=3)
    fine_res = tendency(padded_fine, fine, former, coupling, float(RATIO))
    piece_rows = fine_rows // RATIO
    piece = fine_res.reshape(fields, levels, piece_rows, RATIO, PC, RATIO).mean(axis=(3, 5))
    restricted = gather_directly(piece, "gy", 2)
    target = col_block * block_y + jnp.arange(block_y, dtype=jnp.int32) - start_y
    valid = ((target >= 0) & (target < PC)).astype(jnp.float32)
    placed_block = jnp.take(restricted, jnp.clip(target, 0, PC - 1), axis=3) * valid
    contrib = lax.dynamic_update_slice(
        jnp.zeros((fields, levels, grid_x, block_y), jnp.float32),
        placed_block,
        (zero, zero, start_x, zero),
    )
    covered_sum = lax.psum_scatter(contrib, "gx", scatter_dimension=2, tiled=True)
    rows_here = row_block * block_x + jnp.arange(block_x, dtype=jnp.int32)
    cols_here = col_block * block_y + jnp.arange(block_y, dtype=jnp.int32)
    inside_x = (
        (patch_offsets[:, 0:1] <= rows_here[None, :])
        & (rows_here[None, :] < patch_offsets[:, 0:1] + PC)
    ).astype(jnp.float32)
    inside_y = (
        (patch_offsets[:, 1:2] <= cols_here[None, :])
        & (cols_here[None, :] < patch_offsets[:, 1:2] + PC)
    ).astype(jnp.float32)
    covered = jnp.dot(inside_x.T, inside_y, precision=lax.Precision.HIGHEST) > 0.5
    base_out = jnp.where(covered[None, None], covered_sum, base_tend)
    base_sq = jnp.sum(jnp.where(covered[None, None], 0.0, base_tend * base_tend))
    fine_sq = jnp.sum(fine_res * fine_res) / (RATIO * RATIO)
    totals = lax.psum((base_sq, fine_sq), ("gx", "gy"))
    residual_norm = jnp.sqrt(totals[0] + totals[1])
    return (base_out, fine_res[:, :, None], residual_norm)


def solution(mesh):
    placed = (
        P(None, None, "gx", "gy"),
        P(None, None, "gx", "gy"),
        P(None, None, "gx", "gy", None),
        P(None, None, "gx", "gy", None),
        P(),
        P(),
        P(),
    )
    return jax.shard_map(
        local,
        mesh=mesh,
        in_specs=placed,
        out_specs=(P(None, None, "gx", "gy"), P(None, None, "gx", "gy", None), P()),
        check_vma=False,
    )
```

profile of v0, /device:TPU:1, one launch (start us, length us, event | category | flops | bytes accessed | tf_op | source)
XLA Modules:
  0.0 299.0 jit_solution(7654715995764800030)
XLA Ops:
  7.2 0.7 fusion.5
  7.9 0.8 multiply_reduce_fusion.1
  9.1 1.9 copy.267
  11.0 1.4 gather_fusion.1
  12.4 1.2 copy.268
  14.2 1.7 gather_fusion
  17.0 24.2 %all_to_all.10 = f32[16,4,8,2,192]{4,3,2,1,0:T(2,128)S(1)} all-to-all(f32[16,4,8,2,192]{4,3,2,1,0:T(2,128)S(1)} %pad_maximum_fusion.18), channel_id=1, replica_groups=mesh['gx'=16,'gy'=8] {'gx'}, dimensions={0} | all-to-all | bytes 1572864 | tf_op jit(solution)/shard_map/all_to_all | solution.py:31
  41.9 0.7 pad_maximum_fusion.19
  42.7 1.5 copy.344
  44.3 3.8 %collective-permute-start = (f32[4,8,1,264]{3,1,2,0:T(8,128)S(1)}, f32[4,8,1,264]{3,1,2,0:T(8,128)S(1)}, u32[]{:S(2)}, u32[]{:S(2)}) collective-permute-start(f32[4,8,1,264]{3,1,2,0:T(8,128)S(1)} %get-tuple-element.38), channel_id=1, source_target_pairs={{1,0},{2,1},{3,2},{4,3},{5,4},{6,5},{7,6},{9,8},{10,9},{11,10},{12... | collective-permute-start | bytes 101384 | tf_op jit(solution)/shard_map/ppermute | solution.py:23
  48.1 3.3 %collective-permute-start.1 = (f32[4,8,1,264]{3,1,2,0:T(8,128)S(1)}, f32[4,8,1,264]{3,1,2,0:T(8,128)S(1)}, u32[]{:S(2)}, u32[]{:S(2)}) collective-permute-start(f32[4,8,1,264]{3,1,2,0:T(8,128)S(1)} %get-tuple-element.37), channel_id=1, source_target_pairs={{0,1},{1,2},{2,3},{3,4},{4,5},{5,6},{6,7},{8,9},{9,10},{10,11},{11... | collective-permute-start | bytes 101384 | tf_op jit(solution)/shard_map/ppermute | solution.py:20
  53.1 0.7 fusion.26
  54.1 1.3 slice_bitcast_fusion.4
  55.4 1.9 fusion.31
  57.3 0.7 compare_and_fusion
  58.2 1.0 copy.275
  59.2 9.2 %all-gather.3.cloned.1.call-done = f32[589824]{0:T(1024)} async-done(((f32[73728]{0:T(1024)}), f32[589824]{0:T(1024)}) %all-gather.3.cloned.1.call-update) | async-done | bytes 2359312 | tf_op jit(solution)/shard_map/all_gather | solution.py:49
  68.4 3.5 %reshape.361 = f32[8,73728]{1,0:T(8,128)} reshape(f32[589824]{0:T(1024)} %all-gather.3.cloned.1.call-done) | data formatting | bytes 4718592 | tf_op jit(solution)/shard_map/all_gather | solution.py:49
  71.9 2.9 slice_reduce_fusion
  74.8 1.0 reshape.317
  75.7 4.3 %copy.272 = f32[4,8,2,8,128]{1,0,4,3,2:T(4,128)} copy(f32[4,8,2,8,128]{4,2,1,0,3:T(2,128)} %bitcast.89) | data formatting | bytes 524288 | tf_op jit(solution)/shard_map/transpose | solution.py:42
  80.0 4.6 %gather_fusion.2 = f32[264,4,8,2]{2,1,3,0:T(4,128)} fusion(f32[4,8,2,1024]{1,0,3,2:T(4,128)} %bitcast.86, s32[1024]{0:T(1024)S(1)} %pad_clamp_fusion.2), kind=kCustom, calls=%fused_computation.2 | custom fusion | bytes 136224 | tf_op jit(solution)/shard_map/jit(_take)/gather | solution.py:124
  84.7 2.0 select_bitcast_fusion
  86.7 1.3 slice_select_fusion
  88.0 1.3 copy.274
  89.3 1.3 copy.276
  90.7 3.1 %copy.280 = f32[4,8,2,1024]{1,0,3,2:T(4,128)} copy(f32[4,8,2,1024]{3,2,1,0:T(2,128)S(1)} %reduce_sum.59) | data formatting | bytes 524288 | tf_op jit(solution)/shard_map/reduce_sum | solution.py:122
  93.8 2.8 gather_fusion.3
  96.9 0.9 copy.285
  97.7 1.6 copy.283
  99.4 6.8 %multiply_reduce_fusion = (f32[]{:T(128)}, f32[4,8,33,264]{3,1,2,0:T(8,128)}) fusion(f32[8,33,264]{2,0,1:T(8,128)} %get-tuple-element.36, f32[4]{0:T(128)S(1)} %get-tuple-element.23, f32[8,33,264]{2,0,1:T(8,128)} %get-tuple-element.34, f32[4]{0:T(128)S(1)} %get-tuple-element.24, f32[4]{0:T(128)S(1)} %get-tuple-element.22, f32[4]{0:T(128)S(1)} %get-tuple-element.21, ...), kind=kLoop, calls=%fused_computation.19 | loop fusion | flops 11430143 | bytes 6488516 | tf_op jit(solution)/shard_map/reduce_sum | solution.py:163
  106.2 14.1 %copy.288 = f32[4,8,33,264]{1,0,3,2:T(4,128)} copy(f32[4,8,33,264]{3,1,2,0:T(8,128)} %get-tuple-element.26) | data formatting | bytes 2230272 | tf_op jit(solution)/shard_map/add | solution.py:81
  120.3 12.0 %reduce_sum.60 = f32[4,8,11,88]{1,0,3,2:T(4,128)S(1)} reduce(f32[4,8,11,3,88,3]{1,0,5,4,3,2:T(4,128)} %bitcast.79, f32[]{:T(128)} %constant.62.clone.1), dimensions={3,5}, to_apply=%region_3.4 | reduce | flops 247808 | bytes 1239044 | tf_op jit(solution)/shard_map/reduce_sum | solution.py:139
  132.3 1.5 copy.289
  133.8 1.2 broadcast_in_dim.107
  135.0 3.8 %all-to-all-start.1 = ((f32[8,4,8,11,88]{4,2,3,1,0:T(8,128)}), f32[8,4,8,11,88]{4,2,3,1,0:T(8,128)S(1)}, u32[]{:S(2)}, u32[]{:S(2)}) async-start(f32[8,4,8,11,88]{4,2,3,1,0:T(8,128)} %broadcast_in_dim.107), calls=%async_computation.1 | async-start | bytes 2883584 | tf_op jit(solution)/shard_map/all_to_all | solution.py:59
  142.0 16.0 %all-to-all-done.1 = f32[8,4,8,11,88]{4,2,3,1,0:T(8,128)S(1)} async-done(((f32[8,4,8,11,88]{4,2,3,1,0:T(8,128)}), f32[8,4,8,11,88]{4,2,3,1,0:T(8,128)S(1)}, u32[]{:S(2)}, u32[]{:S(2)}) %all-to-all-start.1) | async-done | bytes 991264 | tf_op jit(solution)/shard_map/all_to_all | solution.py:59
  158.0 1.2 copy.290
  159.2 1.9 copy.291
  161.1 2.2 gather_fusion.4
  163.3 1.9 multiply_bitcast_fusion
  165.2 2.1 copy.292
  167.4 7.9 %broadcast_in_dim.96 = f32[4,8,1024,128]{3,1,0,2:T(8,128)} broadcast(f32[]{:T(128)} %constant.62.clone.1), dimensions={} | broadcast | bytes 16777220 | tf_op jit(solution)/shard_map/broadcast_in_dim | solution.py:145
  175.2 1.2 constant_dynamic-update-slice_fusion
  176.5 1.3 collective-permute-start.2
  177.8 4.0 %collective-permute-start.3 = (f32[4,8,1,128]{3,1,2,0:T(8,128)S(1)}, f32[4,8,1,128]{3,1,2,0:T(8,128)S(1)}, u32[]{:S(2)}, u32[]{:S(2)}) collective-permute-start(f32[4,8,1,128]{3,1,2,0:T(8,128)S(1)} %bitcast.95), channel_id=1, source_target_pairs={{0,8},{8,16},{16,24},{24,32},{32,40},{40,48},{48,56},{56,64},{64,7... | collective-permute-start | bytes 49160 | tf_op jit(solution)/shard_map/ppermute | solution.py:20
  182.4 1.0 slice_bitcast_fusion.8
  183.4 1.2 fusion.34
  184.8 1.4 fusion.32
  186.1 1.9 copy.306
  188.0 3.4 %collective-permute-start.4 = (f32[4,8,66,1]{2,1,3,0:T(8,128)S(1)}, f32[4,8,66,1]{2,1,3,0:T(8,128)S(1)}, u32[]{:S(2)}, u32[]{:S(2)}) collective-permute-start(f32[4,8,66,1]{2,1,3,0:T(8,128)S(1)} %copy.306), channel_id=1, source_target_pairs={{1,0},{2,1},{3,2},{4,3},{5,4},{6,5},{7,6},{9,8},{10,9},{11,10},{12... | collective-permute-start | bytes 25352 | tf_op jit(solution)/shard_map/ppermute | solution.py:23
  191.4 0.7 copy.308
  192.1 2.2 collective-permute-start.5
  194.6 1.1 copy.295
  195.7 1.8 copy.302
  197.5 1.8 copy.314
  199.3 1.8 copy.315
  201.1 1.1 copy.307
  202.2 1.9 copy.309
  204.1 5.9 %select_reduce_fusion = (f32[]{:T(128)}, f32[4,8,64,128]{3,1,0,2:T(8,128)}) fusion(pred[64,128]{1,0:T(8,128)(4,1)S(1)} %convolution_compare_fusion, f32[8,64,128]{2,0,1:T(8,128)} %copy.315, f32[4]{0:T(128)} %copy-done.6, f32[8,64,128]{2,0,1:T(8,128)} %copy.314, f32[4]{0:T(128)} %copy-done.7, f32[4]{0:T(128)S(1)} %get-tuple-element.22, ...), kind=kLoop, calls=%fused_computation.34 | loop fusion | flops 10485759 | bytes 6087236 | tf_op jit(solution)/shard_map/reduce_sum | solution.py:162
  211.2 71.4 %psum.16 = f32[]{:T(128)} all-reduce(f32[]{:T(128)S(6)} %add.389), channel_id=1, replica_groups=mesh['gx'=16,'gy'=8] {'gx','gy'}, use_global_device_ids=true, to_apply=%region_6.7 | all-reduce | flops 1 | bytes 8 | tf_op jit(solution)/shard_map/psum | solution.py:164
  283.3 4.4 %copy.317 = f32[4,8,1,33,264]{4,2,3,1,0:T(1,128)} copy(f32[4,8,1,33,264]{4,1,3,2,0:T(8,128)} %bitcast.83) | data formatting | bytes 2230272
  288.0 1.5 broadcast_select_fusion
  289.5 1.6 copy.316
  (79 shorter events, 8.0 us)
Async XLA Ops:
  7.2 61.2 %all-gather.3.cloned.1.call-start = ((), (), s32[]{:S(2)}) async-start(), calls=%async_computation.4 | async-start | bytes 2654208 | tf_op jit(solution)/shard_map/all_gather | solution.py:49
  12.4 1.8 copy-start
  42.7 11.1 %copy-start.5 = (f32[4,4]{1,0:T(4,128)S(1)}, f32[4,4]{1,0:T(4,128)}, u32[]{:S(2)}) copy-start(f32[4,4]{1,0:T(4,128)} %param.11) | copy-start | bytes 196
  44.3 13.7 %collective-permute-start = (f32[4,8,1,264]{3,1,2,0:T(8,128)S(1)}, f32[4,8,1,264]{3,1,2,0:T(8,128)S(1)}, u32[]{:S(2)}, u32[]{:S(2)}) collective-permute-start(f32[4,8,1,264]{3,1,2,0:T(8,128)S(1)} %get-tuple-element.38), channel_id=1, source_target_pairs={{1,0},{2,1},{3,2},{4,3},{5,4},{6,5},{7,6},{9,8},{10,9},{11,10},{12... | collective-permute-start | bytes 101384 | tf_op jit(solution)/shard_map/ppermute | solution.py:23
  48.1 10.1 %collective-permute-start.1 = (f32[4,8,1,264]{3,1,2,0:T(8,128)S(1)}, f32[4,8,1,264]{3,1,2,0:T(8,128)S(1)}, u32[]{:S(2)}, u32[]{:S(2)}) collective-permute-start(f32[4,8,1,264]{3,1,2,0:T(8,128)S(1)} %get-tuple-element.37), channel_id=1, source_target_pairs={{0,1},{1,2},{2,3},{3,4},{4,5},{5,6},{6,7},{8,9},{9,10},{10,11},{11... | collective-permute-start | bytes 101384 | tf_op jit(solution)/shard_map/ppermute | solution.py:20
  54.1 45.3 %copy-start.6 = (f32[4]{0:T(128)}, f32[4]{0:T(128)S(1)}, u32[]{:S(2)}) copy-start(f32[4]{0:T(128)S(1)} %get-tuple-element.23) | copy-start | bytes 52
  54.1 45.3 %copy-start.7 = (f32[4]{0:T(128)}, f32[4]{0:T(128)S(1)}, u32[]{:S(2)}) copy-start(f32[4]{0:T(128)S(1)} %get-tuple-element.24) | copy-start | bytes 52
  71.9 2.9 slice-start
  84.7 2.1 copy-start.3
  86.7 3.9 %copy-start.4 = (f32[65536]{0:T(1024)S(1)}, f32[65536]{0:T(1024)}, u32[]{:S(2)}) copy-start(f32[65536]{0:T(1024)} %slice_reduce_fusion) | copy-start | bytes 786436
  135.0 23.0 %all-to-all-start.1 = ((f32[8,4,8,11,88]{4,2,3,1,0:T(8,128)}), f32[8,4,8,11,88]{4,2,3,1,0:T(8,128)S(1)}, u32[]{:S(2)}, u32[]{:S(2)}) async-start(f32[8,4,8,11,88]{4,2,3,1,0:T(8,128)} %broadcast_in_dim.107), calls=%async_computation.1 | async-start | bytes 2883584 | tf_op jit(solution)/shard_map/all_to_all | solution.py:59
  138.8 149.1 %reduce-scatter.2.cloned.1.call-start = ((), (), s32[]{:S(2)}) async-start(), calls=%async_computation.3 | async-start | bytes 17825792 | tf_op jit(solution)/shard_map/reduce_scatter | solution.py:149
  167.4 7.9 %copy-start.1 = (f32[4,8,88,128]{3,1,0,2:T(8,128)S(1)}, f32[4,8,88,128]{3,1,0,2:T(8,128)}, u32[]{:S(2)}) copy-start(f32[4,8,88,128]{3,1,0,2:T(8,128)} %copy.292) | copy-start | bytes 4325380
  176.4 6.0 %copy-start.8 = (s32[16,2]{0,1:T(2,128)S(1)}, s32[16,2]{0,1:T(2,128)}, u32[]{:S(2)}) copy-start(s32[16,2]{0,1:T(2,128)} %param.12) | copy-start | bytes 388
  176.5 8.2 %collective-permute-start.2 = (f32[4,8,1,128]{3,1,2,0:T(8,128)S(1)}, f32[4,8,1,128]{3,1,2,0:T(8,128)S(1)}, u32[]{:S(2)}, u32[]{:S(2)}) collective-permute-start(f32[4,8,1,128]{3,1,2,0:T(8,128)S(1)} %bitcast.96), channel_id=1, source_target_pairs={{8,0},{16,8},{24,16},{32,24},{40,32},{48,40},{56,48},{64,56},{72,6... | collective-permute-start | bytes 49160 | tf_op jit(solution)/shard_map/ppermute | solution.py:23
  177.8 6.9 %collective-permute-start.3 = (f32[4,8,1,128]{3,1,2,0:T(8,128)S(1)}, f32[4,8,1,128]{3,1,2,0:T(8,128)S(1)}, u32[]{:S(2)}, u32[]{:S(2)}) collective-permute-start(f32[4,8,1,128]{3,1,2,0:T(8,128)S(1)} %bitcast.95), channel_id=1, source_target_pairs={{0,8},{8,16},{16,24},{24,32},{32,40},{40,48},{48,56},{56,64},{64,7... | collective-permute-start | bytes 49160 | tf_op jit(solution)/shard_map/ppermute | solution.py:20
  188.0 13.1 %collective-permute-start.4 = (f32[4,8,66,1]{2,1,3,0:T(8,128)S(1)}, f32[4,8,66,1]{2,1,3,0:T(8,128)S(1)}, u32[]{:S(2)}, u32[]{:S(2)}) collective-permute-start(f32[4,8,66,1]{2,1,3,0:T(8,128)S(1)} %copy.306), channel_id=1, source_target_pairs={{1,0},{2,1},{3,2},{4,3},{5,4},{6,5},{7,6},{9,8},{10,9},{11,10},{12... | collective-permute-start | bytes 25352 | tf_op jit(solution)/shard_map/ppermute | solution.py:23
  192.1 10.1 %collective-permute-start.5 = (f32[4,8,66,1]{2,1,3,0:T(8,128)S(1)}, f32[4,8,66,1]{2,1,3,0:T(8,128)S(1)}, u32[]{:S(2)}, u32[]{:S(2)}) collective-permute-start(f32[4,8,66,1]{2,1,3,0:T(8,128)S(1)} %copy.308), channel_id=1, source_target_pairs={{0,1},{1,2},{2,3},{3,4},{4,5},{5,6},{6,7},{8,9},{9,10},{10,11},{11... | collective-permute-start | bytes 25352 | tf_op jit(solution)/shard_map/ppermute | solution.py:20
  283.3 4.6 %copy-start.2 = (f32[4,8,64,128]{3,1,0,2:T(8,128)S(1)}, f32[4,8,64,128]{3,1,0,2:T(8,128)}, u32[]{:S(2)}) copy-start(f32[4,8,64,128]{3,1,0,2:T(8,128)} %get-tuple-element.28) | copy-start | bytes 3145732
Sparse Core Ops, SparseCore 0:
  42.8 25.5 all-gather.2
  176.6 111.3 reduce-scatter.1
where the time goes:
time: 301 us; the launch traced here: 299 us
  blocking collectives  95.6 us (32%)
  local copies, waits for them, and re-layouts  94.7 us (31%)
  other arithmetic  41.7 us (14%)
  waiting for transfers between devices  25.6 us (9%)
  starting transfers between devices  21.8 us (7%)
  between operations  19.6 us (7%)
    psum x1, blocking collectives, local(): totals = lax.psum((base_sq, fine_sq), ('gx', 'gy'))  71.4 us
    all_to_all x1, blocking collectives, sent_together(): lax.all_to_all(both, axis, split_axis=split_dim, concat_axis=concat_dim,...  24.2 us
    all_to_all x1, waiting for transfers between devices, sent_to_all(): return lax.all_to_all(copies, axis, split_axis=0, concat_axis=0, tiled=True)  16 us
    add x1, local copies, waits for them, and re-layouts, tendency(): state - former  14.1 us
    reduce_sum x1, other arithmetic, local(): fine_res.reshape(fields, levels, piece_rows, RATIO, PC, RATIO)  12 us
    unnamed x23, local copies, waits for them, and re-layouts  10 us
    ppermute x3, starting transfers between devices, padded_2(): lax.ppermute(lax.slice_in_dim(block, block.shape[dim] - width, None, axis...  9.44 us
    all_gather x1, waiting for transfers between devices, gather_packed(): lines, at, done = (lax.all_gather(vector, axis), 0, [])  9.19 us
  transfers between devices with their start and end apart: 9, of which 3 were waited for; matrix products, arithmetic and copies ran while one was open for 13% of the time, Pallas kernels for 0%

commit v1 on v0

v1 whole, which is shorter than its diff:
```python
import functools

import jax
import jax.numpy as jnp
from jax import lax
from jax.experimental import pallas as pl
from jax.experimental.pallas import tpu as pltpu
from jax.sharding import PartitionSpec as P

PC = 88
NG, NM = 16, 8
BX, BY = 64, 128
FR, FC = 33, 264
MESH = pl.DeviceIdType.MESH
VM = pltpu.VMEM
F32 = jnp.float32
HI = lax.Precision.HIGHEST


def vspec():
    return pl.BlockSpec(memory_space=pltpu.VMEM)


def sspec():
    return pl.BlockSpec(memory_space=pltpu.SMEM)


def shape(*dims):
    return jax.ShapeDtypeStruct(dims, F32)


def iota(dims, axis):
    return lax.broadcasted_iota(jnp.int32, dims, axis)


def extract_kernel(off, pg, base, fine, pxy, s1, hr, hc, fh, trans):
    r = lax.axis_index("gx")
    c = lax.axis_index("gy")
    for p in range(NG):
        g = pg[p]
        pxy[0, g] = off[p, 0]
        pxy[1, g] = off[p, 1]
    for q in range(16):
        trans[pl.ds(q, 128, stride=16), :] = base[pl.ds(128 * q, 128), :].T
    hr[0] = base[pl.ds(0, 32, stride=BX), :]
    hr[1] = base[pl.ds(BX - 1, 32, stride=BX), :]
    hc[0] = trans[pl.ds(0, 16), :]
    hc[1] = trans[pl.ds(127 * 16, 16), :]
    zero = jnp.zeros((32, 384 - FC), F32)
    fh[0] = jnp.concatenate([fine[:, 0, :], zero], axis=1)
    fh[1] = jnp.concatenate([fine[:, FR - 1, :], zero], axis=1)

    def body(g, _):
        x = pxy[0, g]
        y = pxy[1, g]
        lo = x - 1 - r * BX
        hi = x + PC - r * BX
        loc = jnp.where((lo >= 0) & (lo < BX), lo, jnp.clip(hi, 0, BX - 1))
        s1[g, 0:32, :] = base[pl.ds(loc, 32, stride=BX), :]
        y0 = jnp.clip(y - 1 - c * BY, 0, BY - 1)
        s1[g, 32:48, :] = trans[pl.ds(pl.multiple_of(y0 * 16, 16), 16), :]
        y1 = jnp.clip(y + PC - c * BY, 0, BY - 1)
        s1[g, 48:64, :] = trans[pl.ds(pl.multiple_of(y1 * 16, 16), 16), :]
        return 0

    lax.fori_loop(0, NG, body, 0)


def extract(off, pg, base, fine):
    return pl.pallas_call(
        extract_kernel,
        out_shape=(
            jax.ShapeDtypeStruct((2, NG), jnp.int32),
            shape(NG, 64, 128),
            shape(2, 32, 128),
            shape(2, 16, 128),
            shape(2, 32, 384),
        ),
        in_specs=[sspec(), sspec(), vspec(), vspec()],
        out_specs=(sspec(), vspec(), vspec(), vspec(), vspec()),
        scratch_shapes=[VM((2048, 128), F32)],
    )(off, pg, base, fine)


def wrap(v, n):
    return jnp.where(v >= n, v - n, v)


def here():
    return lax.axis_index("gx"), lax.axis_index("gy")


def gx_peers(gx):
    x = gx // 4
    z = gx - 4 * x
    out = []
    for dx, dz in ((2, 2), (1, 2), (2, 1), (3, 2), (2, 3), (1, 1), (3, 3), (1, 3), (3, 1), (2, 0), (0, 2), (1, 0), (0, 1), (3, 0), (0, 3)):
        out.append(wrap(x + dx, 4) * 4 + wrap(z + dz, 4))
    return out


def gy_peers(gy):
    return [wrap(gy + d, NM) for d in range(1, NM)]


def remote(src, dst, send, recv, a, b):
    return pltpu.make_async_remote_copy(
        src_ref=src, dst_ref=dst, send_sem=send, recv_sem=recv, device_id=(a, b), device_id_type=MESH
    )


def wait_bytes(ref, sem):
    pltpu.make_async_copy(ref, ref, sem).wait()


def cycle_kernel(pxy, s1, hr, hc, fh, gr, tr, br, hrn, hcn, fhn, r1, gs, tb, sa, sb, sc, lsem):
    gx, gy = here()
    bar = pltpu.get_barrier_semaphore()
    ga = gx_peers(gx)
    gb = gy_peers(gy)
    for a in ga:
        pl.semaphore_signal(bar, inc=1, device_id=(a, gy), device_id_type=MESH)
    for b in gb:
        pl.semaphore_signal(bar, inc=1, device_id=(gx, b), device_id_type=MESH)
    own = pltpu.make_async_copy(s1.at[gx], r1.at[gx], lsem.at[0])
    own.start()
    pl.semaphore_wait(bar, len(ga) + len(gb))
    for a in ga:
        remote(s1.at[a], r1.at[gx], sa.at[0], sa.at[1], a, gy).start()
    up, down = wrap(gx + 1, NG), wrap(gx + NG - 1, NG)
    right, left = wrap(gy + 1, NM), wrap(gy + NM - 1, NM)
    halos = [
        remote(hr.at[1], hrn.at[0], sb.at[0], sb.at[1], up, gy),
        remote(hr.at[0], hrn.at[1], sb.at[2], sb.at[3], down, gy),
        remote(hc.at[1], hcn.at[0], sb.at[4], sb.at[5], gx, right),
        remote(hc.at[0], hcn.at[1], sb.at[6], sb.at[7], gx, left),
        remote(fh.at[1], fhn.at[0], sb.at[8], sb.at[9], gx, right),
        remote(fh.at[0], fhn.at[1], sb.at[10], sb.at[11], gx, left),
    ]
    for h in halos:
        h.start()
    own.wait()
    wait_bytes(r1.at[pl.ds(0, NG - 1)], sa.at[1])
    x = pxy[0, gx]
    tb[0] = r1[jnp.maximum(x - 1, 0) // BX, 0:32, :]
    tb[1] = r1[(x + PC) // BX, 0:32, :]
    for j in range(NM):
        a = (x + 11 * j) // BX
        b = jnp.minimum(a + 1, NG - 1)
        gs[j, 0:32, :] = r1[a, 32:64, :]
        gs[j, 32:64, :] = r1[b, 32:64, :]
    for b in gb:
        remote(gs.at[b], gr.at[gy], sc.at[0], sc.at[1], gx, b).start()
    mine = pltpu.make_async_copy(gs.at[gy], gr.at[gy], lsem.at[1])
    mine.start()
    for k, (ref, target) in enumerate(((tr, 0), (br, NM - 1))):
        far = remote(tb.at[k], ref.at[gy], sc.at[2 + 2 * k], sc.at[3 + 2 * k], gx, target)
        near = pltpu.make_async_copy(tb.at[k], ref.at[gy], lsem.at[2])

        @pl.when(gy != target)
        def _():
            far.start()
            far.wait_send()

        @pl.when(gy == target)
        def _():
            near.start()
            near.wait()
            wait_bytes(ref.at[pl.ds(0, NM - 1)], sc.at[3 + 2 * k])

    mine.wait()
    for h in halos:
        h.wait()
    wait_bytes(gr.at[pl.ds(0, NM - 1)], sc.at[1])
    wait_bytes(gr.at[pl.ds(0, NM - 1)], sc.at[0])
    wait_bytes(r1.at[pl.ds(0, NG - 1)], sa.at[0])


def cycle(pxy, s1, hr, hc, fh):
    return pl.pallas_call(
        cycle_kernel,
        out_shape=(
            shape(NM, 64, 128),
            shape(NM, 32, 128),
            shape(NM, 32, 128),
            shape(2, 32, 128),
            shape(2, 16, 128),
            shape(2, 32, 384),
        ),
        in_specs=[sspec()] + [vspec()] * 4,
        out_specs=(vspec(),) * 6,
        scratch_shapes=[
            VM((NG, 64, 128), F32),
            VM((NM, 64, 128), F32),
            VM((2, 32, 128), F32),
            pltpu.SemaphoreType.DMA((2,)),
            pltpu.SemaphoreType.DMA((12,)),
            pltpu.SemaphoreType.DMA((6,)),
            pltpu.SemaphoreType.DMA((3,)),
        ],
        compiler_params=pltpu.CompilerParams(collective_id=0, has_side_effects=True),
    )(pxy, s1, hr, hc, fh)


def stencil(q, north, south, east, west, above, below, old, cpl, a0m, a0p, a1m, a1p, own, f):
    total = own * q[f] - old
    total += north * a0m - south * a0p
    total += east * a1m - west * a1p
    total -= 0.05 * (above + below)
    for g in range(4):
        total += cpl[f][g] * q[g]
    return total


def couplings(cp):
    return [[0.1 * cp[f, g] for g in range(4)] for f in range(4)]


def base_kernel(pxy, cp, base, old, hrn, hcn, tend, psum, hz):
    r = lax.axis_index("gx")
    c = lax.axis_index("gy")
    cpl = couplings(cp)
    keep = [
        jnp.where(r > 0, 1.0, 0.0),
        jnp.where(r < NG - 1, 1.0, 0.0),
        jnp.where(c > 0, 1.0, 0.0),
        jnp.where(c < NM - 1, 1.0, 0.0),
    ]
    hz[0] = hrn[0] * keep[0]
    hz[1] = hrn[1] * keep[1]
    zeros = jnp.zeros((112, 128), F32)
    westc = jnp.concatenate([hcn[0] * keep[2], zeros], axis=0).T
    eastc = jnp.concatenate([hcn[1] * keep[3], zeros], axis=0).T
    row = iota((BX, BY), 0)
    lane = iota((BX, BY), 1)
    open_ = jnp.ones((BX, BY), F32)
    for g in range(NG):
        x = pxy[0, g] - r * BX
        y = pxy[1, g] - c * BY
        inside = (row >= x) & (row < x + PC) & (lane >= y) & (lane < y + PC)
        open_ = jnp.where(inside, 0.0, open_)
    k = 0.02
    own = 1.0 + 4 * k + 0.1
    acc = jnp.zeros((BX, BY), F32)
    for l in range(8):
        q = [base[f * 8 + l] for f in range(4)]
        a0 = 0.05 * q[0]
        a1 = 0.05 * q[1]
        for f in range(4):
            p = f * 8 + l
            pair, par = p // 2, p % 2
            north = jnp.where(row == BX - 1, hz[1, p : p + 1, :], pltpu.roll(q[f], BX - 1, 0))
            south = jnp.where(row == 0, hz[0, p : p + 1, :], pltpu.roll(q[f], 1, 0))
            ecol = pltpu.roll(eastc[par * 64 : par * 64 + 64], 127 - pair, 1)
            wcol = pltpu.roll(westc[par * 64 : par * 64 + 64], (128 - pair) % 128, 1)
            east = jnp.where(lane == BY - 1, ecol, pltpu.roll(q[f], BY - 1, 1))
            west = jnp.where(lane == 0, wcol, pltpu.roll(q[f], 1, 1))
            above = base[p + 1] if l < 7 else jnp.zeros((BX, BY), F32)
            below = base[p - 1] if l > 0 else jnp.zeros((BX, BY), F32)
            total = stencil(
                q, north, south, east, west, above, below, old[p], cpl, a0 - k, a0 + k, a1 - k, a1 + k, own, f
            )
            tend[p] = total
            acc = acc + open_ * (total * total)
    psum[...] = acc.reshape(8, 8, 128).sum(axis=0)


def base_tendency(pxy, cp, base, old, hrn, hcn):
    return pl.pallas_call(
        base_kernel,
        out_shape=(shape(32, BX, BY), shape(8, 128)),
        in_specs=[sspec(), sspec()] + [vspec()] * 4,
        out_specs=(vspec(), vspec()),
        scratch_shapes=[VM((2, 32, 128), F32)],
    )(pxy, cp, base, old, hrn, hcn)


def fine_kernel(pxy, cp, fine, old, fhn, gr, tr, br, bsum, out, ro, pad, hrow, res, mm):
    g = lax.axis_index("gx")
    j = lax.axis_index("gy")
    x = pxy[0, g]
    y = pxy[1, g]
    cpl = couplings(cp)
    first = lax.rem(x + 11 * j, BX)
    cl = (y - 1) // BY
    cr = (y + PC) // BY
    blank = jnp.zeros((96, 128), F32)
    va = jnp.concatenate([gr[cl, 0:16, :], gr[cr, 16:32, :], blank], axis=0)
    vb = jnp.concatenate([gr[cl, 32:48, :], gr[cr, 48:64, :], blank], axis=0)
    want = first + iota((40, 128), 0) // 3
    lane40 = iota((40, 128), 1)
    cols = []
    for par in range(2):
        at = lane40 - 64 * par
        good = (at >= 0) & (at < 64)
        pa = jnp.where(good & (at == want), 1.0, 0.0)
        pb = jnp.where(good & (at + 64 == want), 1.0, 0.0)
        dims = (((1,), (1,)), ((), ()))
        cols.append(
            lax.dot_general(pa, va, dims, precision=HI, preferred_element_type=F32)
            + lax.dot_general(pb, vb, dims, precision=HI, preferred_element_type=F32)
        )
    hrow[0] = fhn[0]
    hrow[1] = fhn[1]

    def spread(cells):
        c0 = y // BY
        c1 = jnp.minimum(c0 + 1, NM - 1)
        b = iota((128, 384), 0)
        jf = iota((128, 384), 1)
        cell = y + jf // 3 - c0 * BY
        good = jf < FC
        p0 = jnp.where(good & (b == cell), 1.0, 0.0)
        p1 = jnp.where(good & (b + BY == cell), 1.0, 0.0)
        return jnp.dot(cells[c0], p0, precision=HI, preferred_element_type=F32) + jnp.dot(
            cells[c1], p1, precision=HI, preferred_element_type=F32
        )

    @pl.when(j == 0)
    def _():
        hrow[0] = spread(tr)

    @pl.when(j == NM - 1)
    def _():
        hrow[1] = spread(br)

    lane33 = iota((FR, 128), 1)
    for f in range(4):
        pad[f * 10] = jnp.zeros((56, 384), F32)
        pad[f * 10 + 9] = jnp.zeros((56, 384), F32)

    def fill(pair, _):
        for par in range(2):
            p = 2 * pair + par
            dst = p + 2 * (p // 8) + 1
            pad[dst, 8 : 8 + FR, 0:256] = fine[p, :, 0:256]
            t = jnp.concatenate([fine[p, :, 256:FC], jnp.zeros((FR, 120), F32)], axis=1)
            cv = cols[par][:FR]
            t = jnp.where(lane33 == 127, pltpu.roll(cv, 127 - pair, 1), t)
            t = jnp.where(lane33 == 8, pltpu.roll(cv, 120 - pair, 1), t)
            pad[dst, 8 : 8 + FR, 256:384] = t
            pad[dst, 7:8, :] = hrow[0, pl.ds(p, 1), :]
            pad[dst, 8 + FR : 9 + FR, :] = hrow[1, pl.ds(p, 1), :]
        return 0

    lax.fori_loop(0, 16, fill, 0)
    k = 0.02 * 9
    own = 1.0 + 4 * k + 0.1

    def level(l, acc):
        for start, n in ((0, 8), (8, 8), (16, 8), (24, 8), (32, 1)):
            s = 8 + start
            q = [pad[f * 10 + 1 + l, s : s + n, :] for f in range(4)]
            a0 = 0.15 * q[0]
            a1 = 0.15 * q[1]
            keep = iota((n, 384), 1) < FC
            for f in range(4):
                z = f * 10 + 1 + l
                north = pad[z, s + 1 : s + 1 + n, :]
                south = pad[z, s - 1 : s - 1 + n, :]
                east = pltpu.roll(q[f], 383, 1)
                west = pltpu.roll(q[f], 1, 1)
                p = f * 8 + l
                before = old[p, start : start + n, :]
                before = jnp.concatenate([before, jnp.zeros((n, 384 - FC), F32)], axis=1)
                total = stencil(
                    q, north, south, east, west, pad[z + 1, s : s + n, :], pad[z - 1, s : s + n, :],
                    before, cpl, a0 - k, a0 + k, a1 - k, a1 + k, own, f,
                )
                out[p, start : start + n, :] = total[:, :FC]
                total = jnp.where(keep, total, 0.0)
                for t in range(3):
                    part = total[:, 128 * t : 128 * t + 128]
                    res[f, t, start : start + n, :] = part
                    sq = part * part
                    if n == 1:
                        sq = jnp.where(iota((8, 128), 0) == 0, jnp.broadcast_to(sq, (8, 128)), 0.0)
                    acc = acc + sq
        for f in range(4):
            for t in range(3):
                rows = [res[f, t, pl.ds(d, 11, stride=3), :] for d in range(3)]
                mm[t, f * 8 + l, 0:11, :] = rows[0] + rows[1] + rows[2]
        return acc

    for t in range(3):
        mm[t, :, 8:16, :] = jnp.zeros((32, 8, 128), F32)
    acc = lax.fori_loop(0, 8, level, jnp.zeros((8, 128), F32))
    total = 0.0
    for t in range(3):
        comb = jnp.where((iota((128, 128), 0) + 128 * t) // 3 == iota((128, 128), 1), 1.0, 0.0)
        total = total + jnp.dot(mm[t].reshape(512, 128), comb, precision=HI, preferred_element_type=F32)
    total = (total * (1.0 / 9.0)).reshape(32, 16, 128)
    norm = bsum[...] + acc * (1.0 / 9.0)
    norm = jnp.sum(norm, axis=0, keepdims=True)
    for i in range(16):
        ro[i, 0:11, :] = total[2 * i, 0:11, :]
        ro[i, 11:22, :] = total[2 * i + 1, 0:11, :]
        ro[i, 22:23, :] = norm
        ro[i, 23:24, :] = norm


def fine_residual(pxy, cp, fine, old, fhn, gr, tr, br, bsum):
    return pl.pallas_call(
        fine_kernel,
        out_shape=(shape(32, FR, FC), shape(NG, 24, 128)),
        in_specs=[sspec(), sspec()] + [vspec()] * 7,
        out_specs=(vspec(), vspec()),
        scratch_shapes=[
            VM((40, 56, 384), F32),
            VM((2, 32, 384), F32),
            VM((4, 3, 40, 128), F32),
            VM((3, 32, 16, 128), F32),
        ],
    )(pxy, cp, fine, old, fhn, gr, tr, br, bsum)


def spray_kernel(ro, ri, send, recv, lsem):
    gx, gy = here()
    bar = pltpu.get_barrier_semaphore()
    ga = gx_peers(gx)
    for a in ga:
        pl.semaphore_signal(bar, inc=1, device_id=(a, gy), device_id_type=MESH)
    own = pltpu.make_async_copy(ro.at[gx], ri.at[gx], lsem)
    own.start()
    pl.semaphore_wait(bar, len(ga))
    for a in ga:
        remote(ro.at[a], ri.at[gx], send, recv, a, gy).start()
    own.wait()
    wait_bytes(ri.at[pl.ds(0, NG - 1)], send)
    wait_bytes(ri.at[pl.ds(0, NG - 1)], recv)


def spray(ro):
    return pl.pallas_call(
        spray_kernel,
        out_shape=shape(NG, 24, 128),
        in_specs=[vspec()],
        out_specs=vspec(),
        scratch_shapes=[pltpu.SemaphoreType.DMA] * 3,
        compiler_params=pltpu.CompilerParams(collective_id=1, has_side_effects=True),
    )(ro)


def place_kernel(pxy, ri, so):
    j = lax.axis_index("gy")
    norm = ri[0, 22:23, :]
    for g in range(1, NG):
        norm = norm + ri[g, 22:23, :]
    fill = jnp.broadcast_to(norm, (24, 128))

    def clear(d, _):
        so[d] = fill
        return 0

    lax.fori_loop(0, NG * NM, clear, 0, unroll=8)
    lane = iota((24, 128), 1)
    body = iota((24, 128), 0) < 22

    def patch(g, _):
        x = pxy[0, g] + 11 * j
        y = pxy[1, g]
        ra = x // BX
        rb = (x + 10) // BX
        c0 = y // BY
        shift = y - c0 * BY
        c1 = jnp.minimum(c0 + 1, NM - 1)
        v = pltpu.roll(ri[g], shift, 1)
        m0 = body & (lane >= shift) & (lane < shift + PC)
        m1 = body & (lane < shift + PC - BY)
        for r in (ra, rb):
            for c, m in ((c0, m0), (c1, m1)):
                so[r * NM + c] = jnp.where(m, v, so[r * NM + c])
        return 0

    lax.fori_loop(0, NG, patch, 0)


def place(pxy, ri):
    return pl.pallas_call(
        place_kernel,
        out_shape=shape(NG * NM, 24, 128),
        in_specs=[sspec(), vspec()],
        out_specs=vspec(),
    )(pxy, ri)


def all_peers(gx, gy):
    x = gx // 4
    z = gx - 4 * x
    y = gy // 2
    c = gy - 2 * y
    offs = [(a, b, d, e) for a in range(4) for b in range(4) for d in range(4) for e in range(2)][1:]
    offs.sort(key=lambda o: -sum(min(v, 4 - v) for v in o[:3]))
    xs = [wrap(x + d, 4) for d in range(4)]
    ys = [wrap(y + d, 4) for d in range(4)]
    zs = [wrap(z + d, 4) for d in range(4)]
    cs = [c, 1 - c]
    return [(xs[a] * 4 + zs[d], ys[b] * 2 + cs[e]) for a, b, d, e in offs]


def scatter_kernel(so, ri, send, recv, lsem):
    gx, gy = here()
    me = gx * NM + gy
    bar = pltpu.get_barrier_semaphore()
    peers = all_peers(gx, gy)
    for a, b in peers:
        pl.semaphore_signal(bar, inc=1, device_id=(a, b), device_id_type=MESH)
    own = pltpu.make_async_copy(so.at[me], ri.at[me], lsem)
    own.start()
    pl.semaphore_wait(bar, len(peers))
    for a, b in peers:
        remote(so.at[a * NM + b], ri.at[me], send, recv, a, b).start()
    own.wait()
    wait_bytes(ri.at[pl.ds(0, NG * NM - 1)], send)
    wait_bytes(ri.at[pl.ds(0, NG * NM - 1)], recv)


def scatter(so):
    return pl.pallas_call(
        scatter_kernel,
        out_shape=shape(NG * NM, 24, 128),
        in_specs=[pl.BlockSpec(memory_space=pl.ANY)],
        out_specs=pl.BlockSpec(memory_space=pl.ANY),
        scratch_shapes=[pltpu.SemaphoreType.DMA] * 3,
        compiler_params=pltpu.CompilerParams(collective_id=2, has_side_effects=True),
    )(so)


def merge_kernel(pxy, tend, ri, out, norm, cells):
    r = lax.axis_index("gx")
    c = lax.axis_index("gy")
    for i in range(16):
        for j in range(NM):
            for par in range(2):
                at = 64 + 11 * j
                cells[2 * i + par, at : at + 11, :] = ri[i * NM + j, 11 * par : 11 * par + 11, :]
    out[...] = tend[...]
    row = iota((BX, BY), 0)
    lane = iota((BX, BY), 1)

    def patch(g, _):
        x = pxy[0, g] - r * BX
        y = pxy[1, g] - c * BY

        @pl.when((x < BX) & (x + PC > 0) & (y < BY) & (y + PC > 0))
        def _():
            inside = (row >= x) & (row < x + PC) & (lane >= y) & (lane < y + PC)
            start = 64 - x

            def plane(p, _):
                out[p] = jnp.where(inside, cells[p, pl.ds(start, BX), :], out[p])
                return 0

            lax.fori_loop(0, 32, plane, 0)

        return 0

    lax.fori_loop(0, NG, patch, 0)
    total = ri[0, 22:23, :]
    for j in range(1, NM):
        total = total + ri[j, 22:23, :]
    norm[...] = jnp.sqrt(jnp.sum(total, axis=1, keepdims=True))


def merge(pxy, tend, ri):
    return pl.pallas_call(
        merge_kernel,
        out_shape=(shape(32, BX, BY), shape(1, 1)),
        in_specs=[sspec(), vspec(), vspec()],
        out_specs=(vspec(), vspec()),
        scratch_shapes=[VM((32, 216, 128), F32)],
    )(pxy, tend, ri)


def local(base_state, base_old, fine_state, fine_old, coupling, patch_offsets, patch_group):
    base = base_state.reshape(32, BX, BY)
    old = base_old.reshape(32, BX, BY)
    fine = fine_state.reshape(32, FR, FC)
    fold = fine_old.reshape(32, FR, FC)
    pxy, s1, hr, hc, fh = extract(patch_offsets, patch_group, base.reshape(2048, 128), fine)
    gr, tr, br, hrn, hcn, fhn = cycle(pxy, s1, hr, hc, fh)
    tend, bsum = base_tendency(pxy, coupling, base, old, hrn, hcn)
    fres, ro = fine_residual(pxy, coupling, fine, fold, fhn, gr, tr, br, bsum)
    ri = spray(ro)
    so = place(pxy, ri)
    r2 = scatter(so)
    bout, norm = merge(pxy, tend, r2)
    return (
        bout.reshape(4, 8, BX, BY),
        fres.reshape(4, 8, 1, FR, FC),
        norm.reshape(()),
    )


def solution(mesh):
    placed = (
        P(None, None, "gx", "gy"),
        P(None, None, "gx", "gy"),
        P(None, None, "gx", "gy", None),
        P(None, None, "gx", "gy", None),
        P(),
        P(),
        P(),
    )
    return jax.shard_map(
        local,
        mesh=mesh,
        in_specs=placed,
        out_specs=(P(None, None, "gx", "gy"), P(None, None, "gx", "gy", None), P()),
        check_vma=False,
    )
```

time: 301 us -> 94 us (0.31)
  blocking collectives: 95.6 us -> 0 us
  local copies, waits for them, and re-layouts: 94.7 us -> 10 us
  Pallas kernels: 0 us -> 83.1 us
  other arithmetic: 41.7 us -> 0 us
  waiting for transfers between devices: 25.6 us -> 0 us
  starting transfers between devices: 21.8 us -> 0 us
  between operations: 19.6 us -> 0.67 us
    pallas_call x0 -> x8, Pallas kernels: none -> 83.1 us  [the longest x1 28.2 us: scatter(): pl.pallas_call(scatter_kernel, out_shape=shape(NG * NM, 24, 128), in_spec...]
    psum x1 -> x0, blocking collectives: 71.4 us -> none  [local(): totals = lax.psum((base_sq, fine_sq), ('gx', 'gy'))]
    reduce_sum x6 -> x0, other arithmetic: 28.5 us -> none  [the longest x1 12 us: local(): fine_res.reshape(fields, levels, piece_rows, RATIO, PC, RATIO)]
    all_to_all x1 -> x0, blocking collectives: 24.2 us -> none  [sent_together(): lax.all_to_all(both, axis, split_axis=split_dim, concat_axis=concat_dim,...]
    ppermute x6 -> x0, starting transfers between devices: 17.9 us -> none  [the longest x3 9.44 us: padded_2(): lax.ppermute(lax.slice_in_dim(block, block.shape[dim] - width, None, axis...]
    all_to_all x1 -> x0, waiting for transfers between devices: 16 us -> none  [sent_to_all(): return lax.all_to_all(copies, axis, split_axis=0, concat_axis=0, tiled=True)]
    add x1 -> x0, local copies, waits for them, and re-layouts: 14.1 us -> none  [tendency(): state - former]
    gather x6 -> x0, local copies, waits for them, and re-layouts: 13.9 us -> none  [the longest x1 4.62 us: local(): edges = jnp.take(cycle_rows, across_fine, axis=3)]
  transfers between devices with their start and end apart: 9 -> 0, of which waited for: 3 -> 0; matrix products, arithmetic and copies ran while one was open for 13% -> 0% of each run, Pallas kernels for 0% -> 0%
where the time goes in v1:
time: 94 us; the launch traced here: 93.8 us
  Pallas kernels  83.1 us (88%)
  local copies, waits for them, and re-layouts  10 us (11%)
    pallas_call x1, Pallas kernels, scatter(): pl.pallas_call(scatter_kernel, out_shape=shape(NG * NM, 24, 128), in_spec...  28.2 us
    pallas_call x1, Pallas kernels, cycle(): pl.pallas_call(cycle_kernel, out_shape=(shape(NM, 64, 128), shape(NM, 32,...  23.4 us
    pallas_call x1, Pallas kernels, spray(): pl.pallas_call(spray_kernel, out_shape=shape(NG, 24, 128), in_specs=[vspe...  8.61 us
    pallas_call x1, Pallas kernels, fine_residual(): pl.pallas_call(fine_kernel, out_shape=(shape(32, FR, FC), shape(NG, 24, 1...  8.25 us
    unnamed x4, local copies, waits for them, and re-layouts  5.73 us
    pallas_call x1, Pallas kernels, base_tendency(): pl.pallas_call(base_kernel, out_shape=(shape(32, BX, BY), shape(8, 128)),...  3.93 us
    pallas_call x1, Pallas kernels, extract(): pl.pallas_call(extract_kernel, out_shape=(jax.ShapeDtypeStruct((2, NG), j...  3.59 us
    pallas_call x1, Pallas kernels, merge(): pl.pallas_call(merge_kernel, out_shape=(shape(32, BX, BY), shape(1, 1)),...  3.55 us

profile of v1, /device:TPU:1, one launch (start us, length us, event | category | flops | bytes accessed | tf_op | source)
XLA Modules:
  0.0 93.8 jit_solution(2776770560103467368)
XLA Ops:
  0.6 1.4 %copy.13.off = s32[16,2]{1,0:T(8,128)} copy(s32[16,2]{0,1:T(2,128)} %param.12) | data formatting | bytes 256 | tf_op args[5]
  2.0 2.9 %copy.19 = f32[4,8,1,33,264]{4,3,1,0,2:T(8,128)} copy(f32[4,8,1,33,264]{4,2,3,1,0:T(1,128)} %param.9) | data formatting | bytes 2230272 | tf_op jit(solution)/shard_map/reshape | solution.py:578
  4.9 3.6 %shard_map.94 = (s32[2,16]{1,0:T(2,128)}, f32[16,64,128]{2,1,0:T(8,128)}, f32[2,32,128]{2,1,0:T(8,128)}, f32[2,16,128]{2,1,0:T(8,128)}, f32[2,32,384]{2,1,0:T(8,128)}) custom-call(s32[16,2]{1,0:T(8,128)} %copy.13.off, s32[16]{0:T(128)} %pg.1, f32[2048,128]{1,0:T(8,128)} %bitcast.13, f32[32,33,264]{2,1,0:T(8,128)} %bitcast.10), custom_call_target="tpu_custom_call" | custom-call | tf_op jit(solution)/shard_map/pallas_call | solution.py:70
  8.5 0.0 copy-start
  8.5 23.4 %shard_map.95 = (f32[8,64,128]{2,1,0:T(8,128)}, f32[8,32,128]{2,1,0:T(8,128)}, f32[8,32,128]{2,1,0:T(8,128)}, f32[2,32,128]{2,1,0:T(8,128)}, f32[2,16,128]{2,1,0:T(8,128)}, /*index=5*/f32[2,32,384]{2,1,0:T(8,128)}) custom-call(s32[2,16]{1,0:T(2,128)} %get-tuple-element.20.pxy, f32[16,64,128]{2,1,0:T(8,128)} %get-tuple-element.21.s1, ...), custom_call_target="tpu_custom_call" | custom-call | tf_op jit(solution)/shard_map/pallas_call | solution.py:180
  31.9 3.9 %shard_map.96 = (f32[32,64,128]{2,1,0:T(8,128)}, f32[8,128]{1,0:T(8,128)}) custom-call(s32[2,16]{1,0:T(2,128)} %get-tuple-element.20.pxy, f32[4,4]{1,0:T(4,128)} %cp.3, f32[32,64,128]{2,1,0:T(8,128)} %bitcast.14, f32[32,64,128]{2,1,0:T(8,128)} %bitcast.16, f32[2,32,128]{2,1,0:T(8,128)} %get-tuple-element.25.hrn, f32[2,16,128]{2,1,0:T(8,128)} %get-tuple-element.26.hcn), custom_call_target="tpu_custom_call" | custom-call | tf_op jit(solution)/shard_map/pallas_call | solution.py:269
  35.8 0.0 copy-done
  35.8 1.4 %copy.20 = f32[4,8,1,33,264]{4,3,1,0,2:T(8,128)} copy(f32[4,8,1,33,264]{4,2,3,1,0:T(1,128)S(1)} %copy-done) | data formatting | bytes 2230272 | tf_op jit(solution)/shard_map/reshape | solution.py:579
  37.3 8.2 %shard_map.97 = (f32[32,33,264]{2,1,0:T(8,128)}, f32[16,24,128]{2,1,0:T(8,128)}) custom-call(s32[2,16]{1,0:T(2,128)} %get-tuple-element.20.pxy, f32[4,4]{1,0:T(4,128)} %cp.3, f32[32,33,264]{2,1,0:T(8,128)} %bitcast.11, f32[32,33,264]{2,1,0:T(8,128)} %bitcast.12, f32[2,32,384]{2,1,0:T(8,128)} %get-tuple-element.28.fhn, f32[8,64,128]{2,1,0:T(8,128)} %get-tuple-element.29.gr, ...), custom_call_target="tpu_custom_call" | custom-call | tf_op jit(solution)/shard_map/pallas_call | solution.py:403
  45.5 8.6 %shard_map.98.ri = f32[16,24,128]{2,1,0:T(8,128)} custom-call(f32[16,24,128]{2,1,0:T(8,128)} %get-tuple-element.33.ro), custom_call_target="tpu_custom_call" | custom-call | tf_op jit(solution)/shard_map/pallas_call | solution.py:434
  54.1 4.4 %copy.18 = f32[4,8,1,33,264]{4,2,3,1,0:T(1,128)} copy(f32[4,8,1,33,264]{4,3,1,0,2:T(8,128)} %bitcast.15) | data formatting | bytes 2230272
  58.5 3.5 %shard_map.99.so = f32[128,24,128]{2,1,0:T(8,128)} custom-call(s32[2,16]{1,0:T(2,128)} %get-tuple-element.20.pxy, f32[16,24,128]{2,1,0:T(8,128)} %shard_map.98.ri), custom_call_target="tpu_custom_call" | custom-call | tf_op jit(solution)/shard_map/pallas_call | solution.py:479
  62.0 28.2 %shard_map.100.ri = f32[128,24,128]{2,1,0:T(8,128)} custom-call(f32[128,24,128]{2,1,0:T(8,128)} %shard_map.99.so), custom_call_target="tpu_custom_call" | custom-call | tf_op jit(solution)/shard_map/pallas_call | solution.py:519
  90.2 3.5 %shard_map.101 = (f32[32,64,128]{2,1,0:T(8,128)}, f32[1,1]{1,0:T(1,128)}) custom-call(s32[2,16]{1,0:T(2,128)} %get-tuple-element.20.pxy, f32[32,64,128]{2,1,0:T(8,128)} %get-tuple-element.27.tend, f32[128,24,128]{2,1,0:T(8,128)} %shard_map.100.ri), custom_call_target="tpu_custom_call" | custom-call | tf_op jit(solution)/shard_map/pallas_call | solution.py:566
Async XLA Ops:
  8.5 27.4 %copy-start = (f32[4,8,1,33,264]{4,2,3,1,0:T(1,128)S(1)}, f32[4,8,1,33,264]{4,2,3,1,0:T(1,128)}, u32[]{:S(2)}) copy-start(f32[4,8,1,33,264]{4,2,3,1,0:T(1,128)} %param.10) | copy-start | bytes 3345412

commit v2 on v0

v2 whole, which is shorter than its diff:
```python
import functools

import jax
import jax.numpy as jnp
from jax import lax
from jax.experimental import pallas as pl
from jax.experimental.pallas import tpu as pltpu
from jax.sharding import PartitionSpec as P

PC = 88
NG, NM = 16, 8
BX, BY = 64, 128
FR, FC = 33, 264
MESH = pl.DeviceIdType.MESH
VM = pltpu.VMEM
F32 = jnp.float32
HI = lax.Precision.HIGHEST


def vspec():
    return pl.BlockSpec(memory_space=pltpu.VMEM)


def sspec():
    return pl.BlockSpec(memory_space=pltpu.SMEM)


def shape(*dims):
    return jax.ShapeDtypeStruct(dims, F32)


def iota(dims, axis):
    return lax.broadcasted_iota(jnp.int32, dims, axis)


def wrap(v, n):
    return jnp.where(v >= n, v - n, v)


def gx_peers(gx):
    x = gx // 4
    z = gx - 4 * x
    out = []
    for dx, dz in GX_OFFSETS:
        out.append(wrap(x + dx, 4) * 4 + wrap(z + dz, 4))
    return out


GX_OFFSETS = (
    (2, 2), (1, 2), (2, 1), (3, 2), (2, 3), (1, 1), (3, 3), (1, 3), (3, 1), (2, 0), (0, 2), (1, 0), (0, 1), (3, 0), (0, 3),
)


def gy_peers(gy):
    return [wrap(gy + d, NM) for d in range(1, NM)]


def all_peers(gx, gy):
    x = gx // 4
    z = gx - 4 * x
    y = gy // 2
    c = gy - 2 * y
    offs = [(a, b, d, e) for a in range(4) for b in range(4) for d in range(4) for e in range(2)][1:]
    offs.sort(key=lambda o: -sum(min(v, 4 - v) for v in o[:3]))
    xs = [wrap(x + d, 4) for d in range(4)]
    ys = [wrap(y + d, 4) for d in range(4)]
    zs = [wrap(z + d, 4) for d in range(4)]
    cs = [c, 1 - c]
    return [(xs[a] * 4 + zs[d], ys[b] * 2 + cs[e]) for a, b, d, e in offs]


def remote(src, dst, send, recv, a, b):
    return pltpu.make_async_remote_copy(
        src_ref=src, dst_ref=dst, send_sem=send, recv_sem=recv, device_id=(a, b), device_id_type=MESH
    )


def wait_bytes(ref, sem):
    pltpu.make_async_copy(ref, ref, sem).wait()


def slot(d, n, size=None):
    return pl.ds(pl.multiple_of(d * n, n), size or n)


def stencil(q, north, south, east, west, above, below, old, cpl, a0m, a0p, a1m, a1p, own, f):
    total = own * q[f] - old
    total += north * a0m - south * a0p
    total += east * a1m - west * a1p
    total -= 0.05 * (above + below)
    for g in range(4):
        total += cpl[f][g] * q[g]
    return total


def couplings(cp):
    return [[0.1 * cp[f, g] for g in range(4)] for f in range(4)]


KB = 0.02
KF = 0.02 * 9


def place_patches(off, pg, pxy):
    for g in range(NG):
        x = jnp.int32(0)
        y = jnp.int32(0)
        for p in range(NG):
            hit = pg[p] == g
            x = x + jnp.where(hit, off[0, p], 0)
            y = y + jnp.where(hit, off[1, p], 0)
        pxy[0, g] = x
        pxy[1, g] = y


def extract_base(r, c, pxy, base, trans, hr, hc, s1):
    flat = trans.reshape(2048, 128)
    for q in range(16):
        flat[pl.ds(q, 128, stride=16), :] = base[2 * q : 2 * q + 2].reshape(128, 128).T
    hr[0] = base[:, 0, :]
    hr[1] = base[:, BX - 1, :]
    hc[0] = trans[0]
    hc[1] = trans[127]

    def body(g, _):
        x = pxy[0, g]
        y = pxy[1, g]
        lo = x - 1 - r * BX
        hi = x + PC - r * BX
        loc = jnp.where((lo >= 0) & (lo < BX), lo, jnp.clip(hi, 0, BX - 1))
        s1[g, 0:32, :] = base[:, loc, :]
        y0 = jnp.clip(y - 1 - c * BY, 0, BY - 1)
        s1[g, 32:48, :] = trans[y0]
        y1 = jnp.clip(y + PC - c * BY, 0, BY - 1)
        s1[g, 48:64, :] = trans[y1]
        return 0

    lax.fori_loop(0, NG, body, 0)


def base_tendency(r, c, pxy, cpl, base, old, hrn, hcn, hz, tend):
    keep = [
        jnp.where(r > 0, 1.0, 0.0),
        jnp.where(r < NG - 1, 1.0, 0.0),
        jnp.where(c > 0, 1.0, 0.0),
        jnp.where(c < NM - 1, 1.0, 0.0),
    ]
    hz[0] = hrn[0] * keep[0]
    hz[1] = hrn[1] * keep[1]
    zeros = jnp.zeros((112, 128), F32)
    westc = jnp.concatenate([hcn[0] * keep[2], zeros], axis=0).T
    eastc = jnp.concatenate([hcn[1] * keep[3], zeros], axis=0).T
    row = iota((BX, BY), 0)
    lane = iota((BX, BY), 1)
    open_ = open_cells(r, c, pxy)
    own = 1.0 + 4 * KB + 0.1
    acc = jnp.zeros((BX, BY), F32)
    for l in range(8):
        q = [base[f * 8 + l] for f in range(4)]
        a0 = 0.05 * q[0]
        a1 = 0.05 * q[1]
        for f in range(4):
            p = f * 8 + l
            pair, par = p // 2, p % 2
            north = jnp.where(row == BX - 1, hz[1, p : p + 1, :], pltpu.roll(q[f], BX - 1, 0))
            south = jnp.where(row == 0, hz[0, p : p + 1, :], pltpu.roll(q[f], 1, 0))
            ecol = pltpu.roll(eastc[par * 64 : par * 64 + 64], 127 - pair, 1)
            wcol = pltpu.roll(westc[par * 64 : par * 64 + 64], (128 - pair) % 128, 1)
            east = jnp.where(lane == BY - 1, ecol, pltpu.roll(q[f], BY - 1, 1))
            west = jnp.where(lane == 0, wcol, pltpu.roll(q[f], 1, 1))
            none = jnp.zeros((BX, BY), F32)
            above = base[p + 1] if l < 7 else none
            below = base[p - 1] if l > 0 else none
            total = stencil(
                q, north, south, east, west, above, below, old[p], cpl,
                a0 - KB, a0 + KB, a1 - KB, a1 + KB, own, f,
            )
            tend[p] = total
            acc = acc + open_ * (total * total)
    return acc.reshape(8, 8, 128).sum(axis=0)


def open_cells(r, c, pxy):
    row = iota((BX, BY), 0)
    lane = iota((BX, BY), 1)
    cells = jnp.ones((BX, BY), F32)
    for g in range(NG):
        x = pxy[0, g] - r * BX
        y = pxy[1, g] - c * BY
        inside = (row >= x) & (row < x + PC) & (lane >= y) & (lane < y + PC)
        cells = jnp.where(inside, 0.0, cells)
    return cells


def fine_interior(cpl, fine, old, pad, res):
    for f in range(4):
        pad[f * 10] = jnp.zeros((56, 384), F32)
        pad[f * 10 + 9] = jnp.zeros((56, 384), F32)

    def fill(p, _):
        dst = p + 2 * (p // 8) + 1
        pad[dst, 0:8, :] = jnp.zeros((8, 384), F32)
        pad[dst, 8 : 8 + FR, 0:256] = fine[p, :, 0:256]
        pad[dst, 8 : 8 + FR, 256:384] = jnp.concatenate([fine[p, :, 256:FC], jnp.zeros((FR, 120), F32)], axis=1)
        pad[dst, 8 + FR : 9 + FR, :] = jnp.zeros((1, 384), F32)
        return 0

    lax.fori_loop(0, 32, fill, 0)
    own = 1.0 + 4 * KF + 0.1

    def level(l, acc):
        for start, n in ((0, 8), (8, 8), (16, 8), (24, 8), (32, 1)):
            s = 8 + start
            q = [pad[f * 10 + 1 + l, s : s + n, :] for f in range(4)]
            a0 = 0.15 * q[0]
            a1 = 0.15 * q[1]
            keep = iota((n, 384), 1) < FC
            for f in range(4):
                z = f * 10 + 1 + l
                north = pad[z, s + 1 : s + 1 + n, :]
                south = pad[z, s - 1 : s - 1 + n, :]
                east = pltpu.roll(q[f], 383, 1)
                west = pltpu.roll(q[f], 1, 1)
                p = f * 8 + l
                before = old[p, start : start + n, :]
                before = jnp.concatenate([before, jnp.zeros((n, 384 - FC), F32)], axis=1)
                total = stencil(
                    q, north, south, east, west, pad[z + 1, s : s + n, :], pad[z - 1, s : s + n, :],
                    before, cpl, a0 - KF, a0 + KF, a1 - KF, a1 + KF, own, f,
                )
                total = jnp.where(keep, total, 0.0)
                for t in range(3):
                    part = total[:, 128 * t : 128 * t + 128]
                    res[pl.ds((t * 32 + p) * 40 + start, n), :] = part
                    sq = part * part
                    if n == 1:
                        sq = jnp.where(iota((8, 128), 0) == 0, jnp.broadcast_to(sq, (8, 128)), 0.0)
                    acc = acc + sq
        return acc

    return lax.fori_loop(0, 8, level, jnp.zeros((8, 128), F32))


def edge_columns(x, y, j, gr):
    first = lax.rem(x + 11 * j, BX)
    cl = jnp.maximum(y - 1, 0) // BY
    cr = (y + PC) // BY
    blank = jnp.zeros((96, 128), F32)
    va = jnp.concatenate([gr[cl, 0:16, :], gr[cr, 16:32, :], blank], axis=0)
    vb = jnp.concatenate([gr[cl, 32:48, :], gr[cr, 48:64, :], blank], axis=0)
    want = first + iota((40, 128), 0) // 3
    lane40 = iota((40, 128), 1)
    cols = []
    for par in range(2):
        at = lane40 - 64 * par
        good = (at >= 0) & (at < 64)
        pa = jnp.where(good & (at == want), 1.0, 0.0)
        pb = jnp.where(good & (at + 64 == want), 1.0, 0.0)
        dims = (((1,), (1,)), ((), ()))
        cols.append(
            lax.dot_general(pa, va, dims, precision=HI, preferred_element_type=F32)
            + lax.dot_general(pb, vb, dims, precision=HI, preferred_element_type=F32)
        )
    return cols


def edge_row(y, cells):
    c0 = y // BY
    c1 = jnp.minimum(c0 + 1, NM - 1)
    b = iota((128, 384), 0)
    jf = iota((128, 384), 1)
    cell = y + jf // 3 - c0 * BY
    good = jf < FC
    p0 = jnp.where(good & (b == cell), 1.0, 0.0)
    p1 = jnp.where(good & (b + BY == cell), 1.0, 0.0)
    return jnp.dot(cells[c0], p0, precision=HI, preferred_element_type=F32) + jnp.dot(
        cells[c1], p1, precision=HI, preferred_element_type=F32
    )


def fine_edges(cols, hrow, fh, fine, res):
    change = jnp.zeros((8, 128), F32)
    for t in range(3):
        for row, side in ((0, 0), (FR - 1, 1)):
            a0 = 0.15 * fh[side, 0:8, 128 * t : 128 * t + 128]
            factor = a0 - KF if side else -(a0 + KF)
            factor = jnp.concatenate([factor] * 4, axis=0)
            at = pl.ds(t * 32 * 40 + row, 32, stride=40)
            was = res[at, :]
            now = was + hrow[side, :, 128 * t : 128 * t + 128] * factor
            res[at, :] = now
            for f in range(4):
                change = change + (now[8 * f : 8 * f + 8] * now[8 * f : 8 * f + 8])
                change = change - (was[8 * f : 8 * f + 8] * was[8 * f : 8 * f + 8])
    lane = iota((FR, 128), 1)
    for l in range(8):
        q1 = fine[8 + l, :, 0:128]
        lo = -(0.15 * q1 + KF)
        q1 = jnp.concatenate([fine[8 + l, :, 256:FC], jnp.zeros((FR, 120), F32)], axis=1)
        hi = 0.15 * q1 - KF
        for f in range(4):
            p = f * 8 + l
            pair, par = p // 2, p % 2
            cv = cols[par][:FR]
            for t, factor, spot, turn in ((0, lo, 0, (128 - pair) % 128), (2, hi, 7, 119 - pair)):
                at = pl.ds((t * 32 + p) * 40, FR)
                was = res[at, :]
                now = jnp.where(lane == spot, was + pltpu.roll(cv, turn, 1) * factor, was)
                res[at, :] = now
                delta = now * now - was * was
                change = change + delta[0:8] + delta[8:16] + delta[16:24] + delta[24:32]
                change = change + jnp.where(iota((8, 128), 0) == 0, jnp.broadcast_to(delta[32:33], (8, 128)), 0.0)
    return change


def restrict(x, j, norm, res, mm, cells, ss):
    for t in range(3):
        mm[t, :, 8:16, :] = jnp.zeros((32, 8, 128), F32)

    def rows(pair, _):
        for par in range(2):
            for t in range(3):
                at = (t * 32 + 2 * pair + par) * 40
                part = [res[pl.ds(at + d, 11, stride=3), :] for d in range(3)]
                mm[t, par * 16 + pair, 0:11, :] = part[0] + part[1] + part[2]
        return 0

    lax.fori_loop(0, 16, rows, 0, unroll=2)
    total = 0.0
    for t in range(3):
        comb = jnp.where((iota((128, 128), 0) + 128 * t) // 3 == iota((128, 128), 1), 1.0, 0.0)
        total = total + jnp.dot(mm[t].reshape(512, 128), comb, precision=HI, preferred_element_type=F32)
    cells[...] = (total * (1.0 / 9.0)).reshape(32, 16, 128)
    lane = iota((16, 128), 1)
    for k in range(NM):
        first = lax.rem(k - x - 11 * j + 2048, 8)
        for par in range(2):
            for h in range(2):
                v = cells[pl.ds(par * 16, 16), first + 8 * h, :]
                if par == 0 and h == 0:
                    v = jnp.where(lane == 127, norm, v)
                ss[pl.ds(k * 8 + par * 2 + h, 16, stride=64), :] = v


def compose(j, pxy, rs, so):
    n = iota((1, 512), 1)
    e = n // 128
    g = (n - e * 128) // 8
    k = n - (n // 8) * 8
    x = jnp.zeros((1, 512), jnp.int32)
    for i in range(NG):
        x = jnp.where(g == i, pxy[0, i], x)
    start = x + 11 * k
    away = j - start + 2048
    first = away - (away // 8) * 8
    h = e - (e // 2) * 2
    row = first + 8 * h
    octet = jnp.where(row <= 10, (start + row - j) // 8, -1)
    take = iota((256, 512), 0)
    par = take // 128
    take = jnp.where((take - par * 128 == octet) & (par == e // 2), 1.0, 0.0)
    lane = iota((8, 128), 1)
    rolled = []
    for i in range(NG):
        y = pxy[1, i]
        shift = lax.rem(y, BY)
        v = [rs[pl.ds(i * 64 + q, 8, stride=8), :] for q in range(4)]
        shift = jnp.broadcast_to(shift, (8, 128))
        for bit in range(7):
            shift, odd = shift // 2, shift - 2 * (shift // 2) == 1
            v = [jnp.where(odd, pltpu.roll(u, 1 << bit, 1), u) for u in v]
        rolled.append(v)
    for c in range(NM):
        parts = [[], [], [], []]
        for i in range(NG):
            at = lane + c * BY - pxy[1, i]
            inside = (at >= 0) & (at < PC)
            for q in range(4):
                parts[q].append(jnp.where(inside, rolled[i][q], 0.0))
        b = jnp.concatenate(parts[0] + parts[1] + parts[2] + parts[3], axis=0)
        got = jnp.dot(take, b, precision=HI, preferred_element_type=F32)
        for r in range(NG):
            for q in range(2):
                so[pl.ds((r * NM + c) * 16 + 8 * q, 8), :] = got[q * 128 + 8 * r : q * 128 + 8 * r + 8]


def main_kernel(
    pxy, cp, base_h, old_h, fine_h, fold_h,
    tend_h, fout_h, norm_h, r2,
    base, old, fine, fold, tend, trans, s1, hr, hc, fh, r1, hrn, hcn, fhn, gs, tb, gr, tr, br, hz,
    pad, hrow, res, mm, cells, ss, rs, so, nv, fout,
    la, sa, sb, sc, sd, se, lb,
):
    gx = lax.axis_index("gx")
    gy = lax.axis_index("gy")
    me = gx * NM + gy
    ga = gx_peers(gx)
    gb = gy_peers(gy)
    peers = all_peers(gx, gy)
    loads = [
        pltpu.make_async_copy(base_h, base, la.at[0]),
        pltpu.make_async_copy(fine_h.at[:, :, 0, :], fine, la.at[1]),
        pltpu.make_async_copy(fold_h.at[:, :, 0, :], fold, la.at[2]),
        pltpu.make_async_copy(old_h, old, la.at[3]),
    ]
    for load in loads:
        load.start()
    bar = pltpu.get_barrier_semaphore()
    for a, b in peers:
        pl.semaphore_signal(bar, inc=1, device_id=(a, b), device_id_type=MESH)
    cpl = couplings(cp)
    loads[0].wait()
    extract_base(gx, gy, pxy, base, trans, hr, hc, s1)
    loads[1].wait()
    blank = jnp.zeros((32, 384 - FC), F32)
    fh[0] = jnp.concatenate([fine[:, 0, :], blank], axis=1)
    fh[1] = jnp.concatenate([fine[:, FR - 1, :], blank], axis=1)
    own = pltpu.make_async_copy(s1.at[gx], r1.at[gx], lb.at[0])
    own.start()
    pl.semaphore_wait(bar, len(peers))

    up, down = wrap(gx + 1, NG), wrap(gx + NG - 1, NG)
    right, left = wrap(gy + 1, NM), wrap(gy + NM - 1, NM)
    halos = [
        remote(hr.at[1], hrn.at[0], sb.at[0], sb.at[1], up, gy),
        remote(hr.at[0], hrn.at[1], sb.at[2], sb.at[3], down, gy),
        remote(hc.at[1], hcn.at[0], sb.at[4], sb.at[5], gx, right),
        remote(hc.at[0], hcn.at[1], sb.at[6], sb.at[7], gx, left),
        remote(fh.at[1], fhn.at[0], sb.at[8], sb.at[9], gx, right),
        remote(fh.at[0], fhn.at[1], sb.at[10], sb.at[11], gx, left),
    ]
    for a in ga:
        remote(s1.at[a], r1.at[gx], sa.at[0], sa.at[1], a, gy).start()
    for h in halos:
        h.start()

    loads[2].wait()
    acc = fine_interior(cpl, fine, fold, pad, res)

    own.wait()
    wait_bytes(r1.at[pl.ds(0, NG - 1)], sa.at[1])
    x = pxy[0, gx]
    y = pxy[1, gx]
    tb[0] = r1[jnp.maximum(x - 1, 0) // BX, 0:32, :]
    tb[1] = r1[(x + PC) // BX, 0:32, :]
    for j in range(NM):
        a = (x + 11 * j) // BX
        b = jnp.minimum(a + 1, NG - 1)
        gs[j, 0:32, :] = r1[a, 32:64, :]
        gs[j, 32:64, :] = r1[b, 32:64, :]
    for b in gb:
        remote(gs.at[b], gr.at[gy], sc.at[0], sc.at[1], gx, b).start()
    mine = pltpu.make_async_copy(gs.at[gy], gr.at[gy], lb.at[1])
    mine.start()
    ends = ((tr, 0, 0), (br, NM - 1, 1))
    for ref, target, k in ends:
        far = remote(tb.at[k], ref.at[gy], sc.at[2 + 2 * k], sc.at[3 + 2 * k], gx, target)
        near = pltpu.make_async_copy(tb.at[k], ref.at[gy], lb.at[2])

        @pl.when(gy != target)
        def _():
            far.start()

        @pl.when(gy == target)
        def _():
            near.start()

    for h in halos:
        h.wait()
    loads[3].wait()
    hrow[0] = fhn[0]
    hrow[1] = fhn[1]
    bsum = base_tendency(gx, gy, pxy, cpl, base, old, hrn, hcn, hz, tend)
    tput = pltpu.make_async_copy(tend, tend_h, lb.at[3])
    tput.start()

    mine.wait()
    wait_bytes(gr.at[pl.ds(0, NM - 1)], sc.at[1])
    for ref, target, k in ends:
        far = remote(tb.at[k], ref.at[gy], sc.at[2 + 2 * k], sc.at[3 + 2 * k], gx, target)
        near = pltpu.make_async_copy(tb.at[k], ref.at[gy], lb.at[2])

        @pl.when(gy != target)
        def _():
            far.wait_send()

        @pl.when(gy == target)
        def _():
            near.wait()
            wait_bytes(ref.at[pl.ds(0, NM - 1)], sc.at[3 + 2 * k])
            hrow[k] = edge_row(y, ref)

    cols = edge_columns(x, y, gy, gr)
    acc = acc + fine_edges(cols, hrow, fh, fine, res)
    norm = jnp.sum(bsum + acc * (1.0 / 9.0), axis=(0, 1), keepdims=True)
    restrict(x, gy, norm, res, mm, cells, ss)
    rs[slot(me, 8), :] = ss[slot(me, 8), :]
    for a, b in peers:
        remote(ss.at[slot(a * NM + b, 8, 4), :], rs.at[slot(me, 8, 4), :], sd.at[0], sd.at[1], a, b).start()

    def write(p, _):
        for t in range(2):
            fout[p, :, 128 * t : 128 * t + 128] = res[pl.ds((t * 32 + p) * 40, FR), :]
        fout[p, :, 256:FC] = res[pl.ds((64 + p) * 40, FR), :][:, 0 : FC - 256]
        return 0

    lax.fori_loop(0, 32, write, 0)
    fput = pltpu.make_async_copy(fout, fout_h, lb.at[4])
    fput.start()

    n = NG * NM - 1
    wait_bytes(rs.at[pl.ds(0, 4 * n), :], sd.at[1])
    compose(gy, pxy, rs, so)
    for a, b in peers:
        remote(so.at[slot(a * NM + b, 16), :], r2.at[slot(me, 16), :], se.at[0], se.at[1], a, b).start()
    keep = pltpu.make_async_copy(so.at[slot(me, 16), :], r2.at[slot(me, 16), :], lb.at[5])
    keep.start()
    total = jnp.sum(rs[pl.ds(0, 128, stride=8), :], axis=0, keepdims=True)
    nv[...] = jnp.broadcast_to(jnp.sqrt(total[:, 127:128]), (8, 128))
    nput = pltpu.make_async_copy(nv, norm_h, lb.at[6])
    nput.start()
    nput.wait()
    keep.wait()
    tput.wait()
    fput.wait()
    wait_bytes(r1.at[pl.ds(0, NG - 1)], sa.at[0])
    wait_bytes(gr.at[pl.ds(0, NM - 1)], sc.at[0])
    wait_bytes(rs.at[pl.ds(0, 4 * n), :], sd.at[0])
    wait_bytes(so.at[pl.ds(0, 16 * n), :], se.at[0])
    wait_bytes(so.at[pl.ds(0, 16 * n), :], se.at[1])


def main(pxy, cp, base, old, fine, fold):
    hbm = pl.BlockSpec(memory_space=pl.ANY)
    dma = pltpu.SemaphoreType.DMA
    return pl.pallas_call(
        main_kernel,
        out_shape=(shape(32, BX, BY), shape(32, FR, FC), shape(8, 128), shape(2048, 128)),
        in_specs=[sspec()] * 2 + [hbm] * 4,
        out_specs=(hbm,) * 4,
        scratch_shapes=[
            VM((32, BX, BY), F32),
            VM((32, BX, BY), F32),
            VM((32, FR, FC), F32),
            VM((32, FR, FC), F32),
            VM((32, BX, BY), F32),
            VM((128, 16, 128), F32),
            VM((NG, 64, 128), F32),
            VM((2, 32, 128), F32),
            VM((2, 16, 128), F32),
            VM((2, 32, 384), F32),
            VM((NG, 64, 128), F32),
            VM((2, 32, 128), F32),
            VM((2, 16, 128), F32),
            VM((2, 32, 384), F32),
            VM((NM, 64, 128), F32),
            VM((2, 32, 128), F32),
            VM((NM, 64, 128), F32),
            VM((NM, 32, 128), F32),
            VM((NM, 32, 128), F32),
            VM((2, 32, 128), F32),
            VM((40, 56, 384), F32),
            VM((2, 32, 384), F32),
            VM((3 * 32 * 40, 128), F32),
            VM((3, 32, 16, 128), F32),
            VM((32, 16, 128), F32),
            VM((1024, 128), F32),
            VM((1024, 128), F32),
            VM((2048, 128), F32),
            VM((8, 128), F32),
            VM((32, FR, FC), F32),
            dma((4,)),
            dma((2,)),
            dma((12,)),
            dma((6,)),
            dma((2,)),
            dma((2,)),
            dma((7,)),
        ],
        compiler_params=pltpu.CompilerParams(collective_id=0, has_side_effects=True),
    )(pxy, cp, base, old, fine, fold)


def merge_kernel(off, tend, ri, fout, nv, out, fres, norm, sem):
    r = lax.axis_index("gx")
    c = lax.axis_index("gy")
    put = pltpu.make_async_copy(fout, fres.at[:, :, 0, :], sem)
    put.start()
    row = iota((8, BY), 0)
    lane = iota((8, BY), 1)
    for t in range(8):
        inside = jnp.zeros((8, BY), jnp.bool_)
        for g in range(NG):
            x = off[0, g] - r * BX - 8 * t
            y = off[1, g] - c * BY
            inside = inside | ((row >= x) & (row < x + PC) & (lane >= y) & (lane < y + PC))
        for p in range(32):
            got = ri[pl.ds((p // 2) * 128 + (p % 2) * 8 + t, 8, stride=16), :]
            out[p, 8 * t : 8 * t + 8, :] = jnp.where(inside, got, tend[p, 8 * t : 8 * t + 8, :])
    norm[...] = nv[0:1, 0:1]
    put.wait()


def merge(off, tend, ri, fout, nv):
    return pl.pallas_call(
        merge_kernel,
        out_shape=(shape(32, BX, BY), shape(32, FR, 1, FC), shape(1, 1)),
        in_specs=[sspec()] + [vspec()] * 4,
        out_specs=(vspec(), pl.BlockSpec(memory_space=pl.ANY), vspec()),
        scratch_shapes=[pltpu.SemaphoreType.DMA],
    )(off, tend, ri, fout, nv)


def local(base_state, base_old, fine_state, fine_old, coupling, patch_offsets, patch_group):
    base = base_state.reshape(32, BX, BY)
    old = base_old.reshape(32, BX, BY)
    fine = fine_state.reshape(32, FR, 1, FC)
    fold = fine_old.reshape(32, FR, 1, FC)
    off = patch_offsets.T
    owner = patch_group[None, :] == jnp.arange(NG, dtype=jnp.int32)[:, None]
    pxy = jnp.sum(jnp.where(owner[None], off[:, None, :], 0), axis=2)
    tend, fout, nv, r2 = main(pxy, coupling, base, old, fine, fold)
    bout, fres, norm = merge(off, tend, r2, fout, nv)
    return (
        bout.reshape(4, 8, BX, BY),
        fres.reshape(4, 8, 1, FR, FC),
        norm.reshape(()),
    )


def solution(mesh):
    placed = (
        P(None, None, "gx", "gy"),
        P(None, None, "gx", "gy"),
        P(None, None, "gx", "gy", None),
        P(None, None, "gx", "gy", None),
        P(),
        P(),
        P(),
    )
    return jax.shard_map(
        local,
        mesh=mesh,
        in_specs=placed,
        out_specs=(P(None, None, "gx", "gy"), P(None, None, "gx", "gy", None), P()),
        check_vma=False,
    )
```

time: 301 us -> 61.2 us (0.20)
  blocking collectives: 95.6 us -> 0 us
  local copies, waits for them, and re-layouts: 94.7 us -> 0 us
  Pallas kernels: 0 us -> 58.3 us
  other arithmetic: 41.7 us -> 2.02 us
  waiting for transfers between devices: 25.6 us -> 0 us
  starting transfers between devices: 21.8 us -> 0 us
  between operations: 19.6 us -> 0.8 us
    psum x1 -> x0, blocking collectives: 71.4 us -> none  [local(): totals = lax.psum((base_sq, fine_sq), ('gx', 'gy'))]
    pallas_call x0 -> x2, Pallas kernels: none -> 58.3 us  [the longest x1 53.9 us: main(): pl.pallas_call(main_kernel, out_shape=(shape(32, BX, BY), shape(32, FR, F...]
    reduce_sum x6 -> x1, other arithmetic: 28.5 us -> 1.36 us  [local(): pxy = jnp.sum(jnp.where(owner[None], off[:, None, :], 0), axis=2)]
    all_to_all x1 -> x0, blocking collectives: 24.2 us -> none  [sent_together(): lax.all_to_all(both, axis, split_axis=split_dim, concat_axis=concat_dim,...]
    ppermute x6 -> x0, starting transfers between devices: 17.9 us -> none  [the longest x3 9.44 us: padded_2(): lax.ppermute(lax.slice_in_dim(block, block.shape[dim] - width, None, axis...]
    all_to_all x1 -> x0, waiting for transfers between devices: 16 us -> none  [sent_to_all(): return lax.all_to_all(copies, axis, split_axis=0, concat_axis=0, tiled=True)]
    add x1 -> x0, local copies, waits for them, and re-layouts: 14.1 us -> none  [tendency(): state - former]
    gather x6 -> x0, local copies, waits for them, and re-layouts: 13.9 us -> none  [the longest x1 4.62 us: local(): edges = jnp.take(cycle_rows, across_fine, axis=3)]
  transfers between devices with their start and end apart: 9 -> 0, of which waited for: 3 -> 0; matrix products, arithmetic and copies ran while one was open for 13% -> 0% of each run, Pallas kernels for 0% -> 0%
where the time goes in v2:
time: 61.2 us; the launch traced here: 61.1 us
  Pallas kernels  58.3 us (95%)
  other arithmetic  2.02 us (3%)
  between operations  0.8 us (1%)
    pallas_call x1, Pallas kernels, main(): pl.pallas_call(main_kernel, out_shape=(shape(32, BX, BY), shape(32, FR, F...  53.9 us
    pallas_call x1, Pallas kernels, merge(): pl.pallas_call(merge_kernel, out_shape=(shape(32, BX, BY), shape(32, FR,...  4.33 us
    reduce_sum x1, other arithmetic, local(): pxy = jnp.sum(jnp.where(owner[None], off[:, None, :], 0), axis=2)  1.36 us

profile of v2, /device:TPU:1, one launch (start us, length us, event | category | flops | bytes accessed | tf_op | source)
XLA Modules:
  0.0 61.1 jit_solution(96841219652185164)
XLA Ops:
  0.6 0.7 %iota_compare_fusion = pred[16,16]{1,0:T(8,128)(4,1)S(1)} fusion(s32[16]{0:T(128)} %param.13), kind=kLoop, calls=%fused_computation.1 | loop fusion | flops 256 | bytes 320 | tf_op jit(solution)/shard_map/eq | solution.py:620
  1.3 1.4 %select_reduce_fusion.pxy = s32[2,16]{1,0:T(2,128)} fusion(s32[2,16]{1,0:T(2,128)} %bitcast.12, pred[16,16]{1,0:T(8,128)(4,1)S(1)} %iota_compare_fusion), kind=kLoop, calls=%fused_computation | loop fusion | flops 992 | bytes 512 | tf_op jit(solution)/shard_map/reduce_sum | solution.py:621
  2.6 53.9 %shard_map.94 = (f32[32,64,128]{2,1,0:T(8,128)}, f32[32,33,264]{2,1,0:T(8,128)}, f32[8,128]{1,0:T(8,128)}, f32[2048,128]{1,0:T(8,128)}) custom-call(s32[2,16]{1,0:T(2,128)} %select_reduce_fusion.pxy, f32[4,4]{1,0:T(4,128)} %cp.1, f32[32,64,128]{2,1,0:T(8,128)} %bitcast.10, f32[32,64,128]{2,1,0:T(8,128)} %bitcast.11, f32[32,33,1,264]{3,2,1,0:T(1,128)} %bitcast.8, ...), custom_call_target="tpu_custom_call" | custom-call | tf_op jit(solution)/shard_map/pallas_call | solution.py:536
  56.6 4.3 %shard_map.95 = (f32[32,64,128]{2,1,0:T(8,128)}, f32[32,33,1,264]{3,2,1,0:T(1,128)}, f32[1,1]{1,0:T(1,128)}) custom-call(s32[2,16]{1,0:T(2,128)} %bitcast.13, f32[32,64,128]{2,1,0:T(8,128)} %get-tuple-element.10.tend, f32[2048,128]{1,0:T(8,128)} %get-tuple-element.11.ri, f32[32,33,264]{2,1,0:T(8,128)} %get-tuple-element.12.fout, f32[8,128]{1,0:T(8,128)} %get-tuple-element.13.nv), custom_call_target="tpu_custom_call" | custom-call | tf_op jit(solution)/shard_map/pallas_call | solution.py:605

commit v3 on v2

--- a/solution.py
+++ b/solution.py
@@ -342,53 +342,75 @@
                 ss[pl.ds(k * 8 + par * 2 + h, 16, stride=64), :] = v
 
 
-def compose(j, pxy, rs, so):
-    n = iota((1, 512), 1)
-    e = n // 128
-    g = (n - e * 128) // 8
+def split3(v):
+    hi = v.astype(jnp.bfloat16)
+    rest = v - hi.astype(F32)
+    mid = rest.astype(jnp.bfloat16)
+    return hi, mid, (rest - mid.astype(F32)).astype(jnp.bfloat16)
+
+
+def compose_send(gx, gy, pxy, rs, so, rolled, take, r2, sems):
+    n = iota((1, 256), 1)
+    h = n // 128
+    g = (n - h * 128) // 8
     k = n - (n // 8) * 8
-    x = jnp.zeros((1, 512), jnp.int32)
+    x = jnp.zeros((1, 256), jnp.int32)
     for i in range(NG):
         x = jnp.where(g == i, pxy[0, i], x)
     start = x + 11 * k
-    away = j - start + 2048
-    first = away - (away // 8) * 8
-    h = e - (e // 2) * 2
-    row = first + 8 * h
-    octet = jnp.where(row <= 10, (start + row - j) // 8, -1)
-    take = iota((256, 512), 0)
-    par = take // 128
-    take = jnp.where((take - par * 128 == octet) & (par == e // 2), 1.0, 0.0)
-    lane = iota((8, 128), 1)
-    rolled = []
+    away = gy - start + 2048
+    row = away - (away // 8) * 8 + 8 * h
+    octet = jnp.where(row <= 10, (start + row - gy) // 8, -1)
+    take[...] = jnp.where(iota((128, 256), 0) == octet, 1.0, 0.0).astype(jnp.bfloat16)
     for i in range(NG):
-        y = pxy[1, i]
-        shift = lax.rem(y, BY)
         v = [rs[pl.ds(i * 64 + q, 8, stride=8), :] for q in range(4)]
-        shift = jnp.broadcast_to(shift, (8, 128))
+        shift = jnp.broadcast_to(lax.rem(pxy[1, i], BY), (8, 128))
         for bit in range(7):
             shift, odd = shift // 2, shift - 2 * (shift // 2) == 1
             v = [jnp.where(odd, pltpu.roll(u, 1 << bit, 1), u) for u in v]
-        rolled.append(v)
-    for c in range(NM):
-        parts = [[], [], [], []]
+        for q in range(4):
+            rolled[q, 8 * i : 8 * i + 8, :] = v[q]
+    lane = iota((8, 128), 1)
+    x4 = gx // 4
+    z4 = gx - 4 * x4
+
+    def column(step, _):
+        c = wrap(gy + step, NM)
+        inside = []
         for i in range(NG):
             at = lane + c * BY - pxy[1, i]
-            inside = (at >= 0) & (at < PC)
-            for q in range(4):
-                parts[q].append(jnp.where(inside, rolled[i][q], 0.0))
-        b = jnp.concatenate(parts[0] + parts[1] + parts[2] + parts[3], axis=0)
-        got = jnp.dot(take, b, precision=HI, preferred_element_type=F32)
-        for r in range(NG):
-            for q in range(2):
-                so[pl.ds((r * NM + c) * 16 + 8 * q, 8), :] = got[q * 128 + 8 * r : q * 128 + 8 * r + 8]
+            inside.append((at >= 0) & (at < PC))
+        for par in range(2):
+            rows = []
+            for q in (2 * par, 2 * par + 1):
+                for i in range(NG):
+                    rows.append(jnp.where(inside[i], rolled[q, 8 * i : 8 * i + 8, :], 0.0))
+            b = jnp.concatenate(split3(jnp.concatenate(rows, axis=0)), axis=1)
+            got = jnp.dot(take[...], b, preferred_element_type=F32)
+            got = got[:, 0:128] + (got[:, 128:256] + got[:, 256:384])
+            for r in range(NG):
+                at = pl.multiple_of((r * NM + c) * 16 + 8 * par, 8)
+                so[pl.ds(at, 8), :] = got[8 * r : 8 * r + 8]
+
+        for dx, dz in GX_OFFSETS + ((0, 0),):
+            a = wrap(x4 + dx, 4) * 4 + wrap(z4 + dz, 4)
+            send = remote(
+                so.at[slot(a * NM + c, 16), :], r2.at[slot(gx * NM + gy, 16), :], sems.at[0], sems.at[1], a, c
+            )
+            if (dx, dz) == (0, 0):
+                pl.when(step > 0)(send.start)
+            else:
+                send.start()
+        return 0
+
+    lax.fori_loop(0, NM, column, 0)
 
 
 def main_kernel(
-    pxy, cp, base_h, old_h, fine_h, fold_h,
+    off, pg, cp, base_h, old_h, fine_h, fold_h,
     tend_h, fout_h, norm_h, r2,
-    base, old, fine, fold, tend, trans, s1, hr, hc, fh, r1, hrn, hcn, fhn, gs, tb, gr, tr, br, hz,
-    pad, hrow, res, mm, cells, ss, rs, so, nv, fout,
+    pxy, base, old, fine, fold, tend, trans, s1, hr, hc, fh, r1, hrn, hcn, fhn, gs, tb, gr, tr, br, hz,
+    pad, hrow, res, mm, cells, ss, rs, so, rolled, take, nv, fout,
     la, sa, sb, sc, sd, se, lb,
 ):
     gx = lax.axis_index("gx")
@@ -406,9 +428,12 @@
     for load in loads:
         load.start()
     bar = pltpu.get_barrier_semaphore()
-    for a, b in peers:
-        pl.semaphore_signal(bar, inc=1, device_id=(a, b), device_id_type=MESH)
+    for a in ga:
+        pl.semaphore_signal(bar, inc=1, device_id=(a, gy), device_id_type=MESH)
+    for b in gb:
+        pl.semaphore_signal(bar, inc=1, device_id=(gx, b), device_id_type=MESH)
     cpl = couplings(cp)
+    place_patches(off, pg, pxy)
     loads[0].wait()
     extract_base(gx, gy, pxy, base, trans, hr, hc, s1)
     loads[1].wait()
@@ -417,7 +442,7 @@
     fh[1] = jnp.concatenate([fine[:, FR - 1, :], blank], axis=1)
     own = pltpu.make_async_copy(s1.at[gx], r1.at[gx], lb.at[0])
     own.start()
-    pl.semaphore_wait(bar, len(peers))
+    pl.semaphore_wait(bar, len(ga) + len(gb))
 
     up, down = wrap(gx + 1, NG), wrap(gx + NG - 1, NG)
     right, left = wrap(gy + 1, NM), wrap(gy + NM - 1, NM)
@@ -510,9 +535,7 @@
 
     n = NG * NM - 1
     wait_bytes(rs.at[pl.ds(0, 4 * n), :], sd.at[1])
-    compose(gy, pxy, rs, so)
-    for a, b in peers:
-        remote(so.at[slot(a * NM + b, 16), :], r2.at[slot(me, 16), :], se.at[0], se.at[1], a, b).start()
+    compose_send(gx, gy, pxy, rs, so, rolled, take, r2, se)
     keep = pltpu.make_async_copy(so.at[slot(me, 16), :], r2.at[slot(me, 16), :], lb.at[5])
     keep.start()
     total = jnp.sum(rs[pl.ds(0, 128, stride=8), :], axis=0, keepdims=True)
@@ -530,15 +553,16 @@
     wait_bytes(so.at[pl.ds(0, 16 * n), :], se.at[1])
 
 
-def main(pxy, cp, base, old, fine, fold):
+def main(off, pg, cp, base, old, fine, fold):
     hbm = pl.BlockSpec(memory_space=pl.ANY)
     dma = pltpu.SemaphoreType.DMA
     return pl.pallas_call(
         main_kernel,
         out_shape=(shape(32, BX, BY), shape(32, FR, FC), shape(8, 128), shape(2048, 128)),
-        in_specs=[sspec()] * 2 + [hbm] * 4,
+        in_specs=[sspec()] * 3 + [hbm] * 4,
         out_specs=(hbm,) * 4,
         scratch_shapes=[
+            pltpu.SMEM((2, NG), jnp.int32),
             VM((32, BX, BY), F32),
             VM((32, BX, BY), F32),
             VM((32, FR, FC), F32),
@@ -567,6 +591,8 @@
             VM((1024, 128), F32),
             VM((1024, 128), F32),
             VM((2048, 128), F32),
+            VM((4, 128, 128), F32),
+            VM((128, 256), jnp.bfloat16),
             VM((8, 128), F32),
             VM((32, FR, FC), F32),
             dma((4,)),
@@ -578,36 +604,79 @@
             dma((7,)),
         ],
         compiler_params=pltpu.CompilerParams(collective_id=0, has_side_effects=True),
-    )(pxy, cp, base, old, fine, fold)
-
-
-def merge_kernel(off, tend, ri, fout, nv, out, fres, norm, sem):
-    r = lax.axis_index("gx")
-    c = lax.axis_index("gy")
-    put = pltpu.make_async_copy(fout, fres.at[:, :, 0, :], sem)
-    put.start()
-    row = iota((8, BY), 0)
-    lane = iota((8, BY), 1)
+    )(off, pg, cp, base, old, fine, fold)
+
+
+PARTS = 4
+
+
+def merge_kernel(off, tend, ri, fout, nv, out, fres, norm, covered, fine, sem):
+    step = pl.program_id(0)
+    piece = 32 // PARTS
+    ins = [
+        pltpu.make_async_copy(fout.at[pl.ds(piece * k, piece)], fine.at[pl.ds(piece * k, piece)], sem.at[k])
+        for k in range(PARTS)
+    ]
+    outs = [
+        pltpu.make_async_copy(fine.at[pl.ds(piece * k, piece)], fres.at[pl.ds(piece * k, piece), :, 0, :], sem.at[PARTS + k])
+        for k in range(PARTS)
+    ]
+
+    @pl.when(step == 0)
+    def _():
+        for copy in ins:
+            copy.start()
+        r = lax.axis_index("gx")
+        c = lax.axis_index("gy")
+        row = iota((BX, BY), 0)
+        lane = iota((BX, BY), 1)
+        inside = jnp.zeros((BX, BY), F32)
+        for g in range(NG):
+            x = off[0, g] - r * BX
+            y = off[1, g] - c * BY
+            inside = jnp.where((row >= x) & (row < x + PC) & (lane >= y) & (lane < y + PC), 1.0, inside)
+        covered[...] = inside
+        norm[...] = nv[0:1, 0:1]
+
     for t in range(8):
-        inside = jnp.zeros((8, BY), jnp.bool_)
-        for g in range(NG):
-            x = off[0, g] - r * BX - 8 * t
-            y = off[1, g] - c * BY
-            inside = inside | ((row >= x) & (row < x + PC) & (lane >= y) & (lane < y + PC))
-        for p in range(32):
+        inside = covered[8 * t : 8 * t + 8, :] > 0.5
+        for p in range(piece):
             got = ri[pl.ds((p // 2) * 128 + (p % 2) * 8 + t, 8, stride=16), :]
             out[p, 8 * t : 8 * t + 8, :] = jnp.where(inside, got, tend[p, 8 * t : 8 * t + 8, :])
-    norm[...] = nv[0:1, 0:1]
-    put.wait()
+
+    for k in range(PARTS):
+
+        @pl.when(step == k)
+        def _():
+            ins[k].wait()
+            outs[k].start()
+
+    @pl.when(step == PARTS - 1)
+    def _():
+        for copy in outs:
+            copy.wait()
 
 
 def merge(off, tend, ri, fout, nv):
+    hbm = pl.BlockSpec(memory_space=pl.ANY)
+    piece = 32 // PARTS
     return pl.pallas_call(
         merge_kernel,
+        grid=(PARTS,),
         out_shape=(shape(32, BX, BY), shape(32, FR, 1, FC), shape(1, 1)),
-        in_specs=[sspec()] + [vspec()] * 4,
-        out_specs=(vspec(), pl.BlockSpec(memory_space=pl.ANY), vspec()),
-        scratch_shapes=[pltpu.SemaphoreType.DMA],
+        in_specs=[
+            sspec(),
+            pl.BlockSpec((piece, BX, BY), lambda i: (i, 0, 0)),
+            pl.BlockSpec((piece * 64, 128), lambda i: (i, 0)),
+            hbm,
+            pl.BlockSpec((8, 128), lambda i: (0, 0)),
+        ],
+        out_specs=(
+            pl.BlockSpec((piece, BX, BY), lambda i: (i, 0, 0)),
+            hbm,
+            pl.BlockSpec((1, 1), lambda i: (0, 0)),
+        ),
+        scratch_shapes=[VM((BX, BY), F32), VM((32, FR, FC), F32), pltpu.SemaphoreType.DMA((2 * PARTS,))],
     )(off, tend, ri, fout, nv)
 
 
@@ -617,9 +686,7 @@
     fine = fine_state.reshape(32, FR, 1, FC)
     fold = fine_old.reshape(32, FR, 1, FC)
     off = patch_offsets.T
-    owner = patch_group[None, :] == jnp.arange(NG, dtype=jnp.int32)[:, None]
-    pxy = jnp.sum(jnp.where(owner[None], off[:, None, :], 0), axis=2)
-    tend, fout, nv, r2 = main(pxy, coupling, base, old, fine, fold)
+    tend, fout, nv, r2 = main(off, patch_group, coupling, base, old, fine, fold)
     bout, fres, norm = merge(off, tend, r2, fout, nv)
     return (
         bout.reshape(4, 8, BX, BY),

time: 61.2 us -> 54.9 us (0.90)
  Pallas kernels: 58.3 us -> 54 us
  other arithmetic: 2.02 us -> 0 us
    pallas_call x1, Pallas kernels: 53.9 us -> 48.3 us  [main(): pl.pallas_call(main_kernel, out_shape=(shape(32, BX, BY), shape(32, FR, F...]
    pallas_call x1, Pallas kernels: 4.33 us -> 5.71 us  [merge(): pl.pallas_call(merge_kernel, grid=(PARTS,), out_shape=(shape(32, BX, BY),...]
    reduce_sum x1 -> x0, other arithmetic: 1.36 us -> none  [local(): pxy = jnp.sum(jnp.where(owner[None], off[:, None, :], 0), axis=2)]
    eq x1 -> x0, other arithmetic: 0.66 us -> none  [local(): owner = patch_group[None, :] == jnp.arange(NG, dtype=jnp.int32)[:, None]]
where the time goes in v3:
time: 54.9 us; the launch traced here: 54.7 us
  Pallas kernels  54 us (98%)
  between operations  0.64 us (1%)
    pallas_call x1, Pallas kernels, main(): pl.pallas_call(main_kernel, out_shape=(shape(32, BX, BY), shape(32, FR, F...  48.3 us
    pallas_call x1, Pallas kernels, merge(): pl.pallas_call(merge_kernel, grid=(PARTS,), out_shape=(shape(32, BX, BY),...  5.71 us

profile of v3, /device:TPU:1, one launch (start us, length us, event | category | flops | bytes accessed | tf_op | source)
XLA Modules:
  0.0 54.7 jit_solution(13274646204341814340)
XLA Ops:
  0.6 48.3 %shard_map.94 = (f32[32,64,128]{2,1,0:T(8,128)}, f32[32,33,264]{2,1,0:T(8,128)}, f32[8,128]{1,0:T(8,128)}, f32[2048,128]{1,0:T(8,128)}) custom-call(s32[2,16]{1,0:T(2,128)} %bitcast.12, s32[16]{0:T(128)} %pg.1, f32[4,4]{1,0:T(4,128)} %cp.1, f32[32,64,128]{2,1,0:T(8,128)} %bitcast.10, f32[32,64,128]{2,1,0:T(8,128)} %bitcast.11, f32[32,33,1,264]{3,2,1,0:T(1,128)} %bitcast.8, ...), custom_call_target="tpu_custom_call" | custom-call | tf_op jit(solution)/shard_map/pallas_call | solution.py:559
  49.0 5.7 %shard_map.95 = (f32[32,64,128]{2,1,0:T(8,128)}, f32[32,33,1,264]{3,2,1,0:T(1,128)}, f32[1,1]{1,0:T(1,128)}) custom-call(s32[2,16]{1,0:T(2,128)} %bitcast.13, f32[32,64,128]{2,1,0:T(8,128)} %get-tuple-element.10.tend, f32[2048,128]{1,0:T(8,128)} %get-tuple-element.11.ri, f32[32,33,264]{2,1,0:T(8,128)} %get-tuple-element.12.fout, f32[8,128]{1,0:T(8,128)} %get-tuple-element.13.nv), custom_call_target="tpu_custom_call" | custom-call | tf_op jit(solution)/shard_map/pallas_call | solution.py:663

commit v4 on v3

--- a/solution.py
+++ b/solution.py
@@ -97,6 +97,8 @@
     return [[0.1 * cp[f, g] for g in range(4)] for f in range(4)]
 
 
+PITCH = 24
+USED = 19
 KB = 0.02
 KF = 0.02 * 9
 
@@ -138,7 +140,7 @@
     lax.fori_loop(0, NG, body, 0)
 
 
-def base_tendency(r, c, pxy, cpl, base, old, hrn, hcn, hz, tend):
+def base_tendency(r, c, pxy, cpl, base, old, hrn, hcn, hz, ring, tend, d0, d1):
     keep = [
         jnp.where(r > 0, 1.0, 0.0),
         jnp.where(r < NG - 1, 1.0, 0.0),
@@ -152,7 +154,7 @@
     eastc = jnp.concatenate([hcn[1] * keep[3], zeros], axis=0).T
     row = iota((BX, BY), 0)
     lane = iota((BX, BY), 1)
-    open_ = open_cells(r, c, pxy)
+    open_ = ring_masks(r, c, pxy, ring)
     own = 1.0 + 4 * KB + 0.1
     acc = jnp.zeros((BX, BY), F32)
     for l in range(8):
@@ -175,20 +177,32 @@
                 q, north, south, east, west, above, below, old[p], cpl,
                 a0 - KB, a0 + KB, a1 - KB, a1 + KB, own, f,
             )
-            tend[p] = total
+            after = ring[1] * north
+            before = ring[0] * south
+            d0[p] = after - before
+            both = after + before
+            after = ring[3] * east
+            before = ring[2] * west
+            d1[p] = after - before
+            tend[p] = open_ * total - (3 * KF / 9) * (both + after + before)
             acc = acc + open_ * (total * total)
     return acc.reshape(8, 8, 128).sum(axis=0)
 
 
-def open_cells(r, c, pxy):
+def ring_masks(r, c, pxy, ring):
     row = iota((BX, BY), 0)
     lane = iota((BX, BY), 1)
     cells = jnp.ones((BX, BY), F32)
+    sides = [jnp.zeros((BX, BY), F32)] * 4
     for g in range(NG):
         x = pxy[0, g] - r * BX
         y = pxy[1, g] - c * BY
         inside = (row >= x) & (row < x + PC) & (lane >= y) & (lane < y + PC)
         cells = jnp.where(inside, 0.0, cells)
+        lines = (row == x, row == x + PC - 1, lane == y, lane == y + PC - 1)
+        sides = [jnp.where(inside & line, 1.0, side) for line, side in zip(lines, sides)]
+    for k in range(4):
+        ring[k] = sides[k]
     return cells
 
 
@@ -278,7 +292,7 @@
     )
 
 
-def fine_edges(cols, hrow, fh, fine, res):
+def fine_rows(hrow, fh, res):
     change = jnp.zeros((8, 128), F32)
     for t in range(3):
         for row, side in ((0, 0), (FR - 1, 1)):
@@ -292,6 +306,11 @@
             for f in range(4):
                 change = change + (now[8 * f : 8 * f + 8] * now[8 * f : 8 * f + 8])
                 change = change - (was[8 * f : 8 * f + 8] * was[8 * f : 8 * f + 8])
+    return change
+
+
+def fine_columns(cols, fine, res):
+    change = jnp.zeros((8, 128), F32)
     lane = iota((FR, 128), 1)
     for l in range(8):
         q1 = fine[8 + l, :, 0:128]
@@ -313,7 +332,7 @@
     return change
 
 
-def restrict(x, j, norm, res, mm, cells, ss):
+def restrict(x, j, fine, fh, qs, res, mm, cells, ss):
     for t in range(3):
         mm[t, :, 8:16, :] = jnp.zeros((32, 8, 128), F32)
 
@@ -327,19 +346,32 @@
 
     lax.fori_loop(0, 16, rows, 0, unroll=2)
     total = 0.0
+    ends = [0.0, 0.0]
     for t in range(3):
         comb = jnp.where((iota((128, 128), 0) + 128 * t) // 3 == iota((128, 128), 1), 1.0, 0.0)
         total = total + jnp.dot(mm[t].reshape(512, 128), comb, precision=HI, preferred_element_type=F32)
+        for side in range(2):
+            row = fh[side, 0:8, 128 * t : 128 * t + 128]
+            ends[side] = ends[side] + jnp.dot(row, comb, precision=HI, preferred_element_type=F32)
     cells[...] = (total * (1.0 / 9.0)).reshape(32, 16, 128)
-    lane = iota((16, 128), 1)
+    for l in range(8):
+        qs[pl.ds(l * 40, FR), :] = fine[8 + l, :, 0:128]
+        qs[pl.ds((8 + l) * 40, FR), :] = jnp.concatenate([fine[8 + l, :, 256:FC], jnp.zeros((FR, 120), F32)], axis=1)
+    lane = iota((11, 128), 1)
+    for l in range(8):
+        for side, turn in ((0, 88), (1, 81)):
+            at = (side * 8 + l) * 40
+            part = [qs[pl.ds(at + d, 11, stride=3), :] for d in range(3)]
+            edge = pltpu.roll(part[0] + part[1] + part[2], turn, 1)
+            cells[2 * l + side, 0:11, :] = jnp.where(lane == 88, edge, cells[2 * l + side, 0:11, :])
     for k in range(NM):
         first = lax.rem(k - x - 11 * j + 2048, 8)
         for par in range(2):
             for h in range(2):
                 v = cells[pl.ds(par * 16, 16), first + 8 * h, :]
-                if par == 0 and h == 0:
-                    v = jnp.where(lane == 127, norm, v)
                 ss[pl.ds(k * 8 + par * 2 + h, 16, stride=64), :] = v
+        for side in range(2):
+            ss[pl.ds((side * 8 + k) * 8 + 4, 8, stride=128), :] = ends[side]
 
 
 def split3(v):
@@ -349,7 +381,7 @@
     return hi, mid, (rest - mid.astype(F32)).astype(jnp.bfloat16)
 
 
-def compose_send(gx, gy, pxy, rs, so, rolled, take, r2, sems):
+def compose_send(gx, gy, pxy, rs, so, rolled, take, turned, r2, sems):
     n = iota((1, 256), 1)
     h = n // 128
     g = (n - h * 128) // 8
@@ -373,6 +405,27 @@
     lane = iota((8, 128), 1)
     x4 = gx // 4
     z4 = gx - 4 * x4
+    side = gx - 2 * (gx // 2)
+    rank = iota((NG, 128), 0)
+    yy = jnp.zeros((NG, 128), jnp.int32)
+    for i in range(NG):
+        yy = jnp.where(rank == i, pxy[1, i], yy)
+    ends = rs[pl.ds(side * (NM - 1) * 8 + 4, NG, stride=64), :]
+    shift = yy - (yy // BY) * BY
+    for bit in range(7):
+        shift, odd = shift // 2, shift - 2 * (shift // 2) == 1
+        ends = jnp.where(odd, pltpu.roll(ends, 1 << bit, 1), ends)
+    spots = []
+    for i in range(NG):
+        spots.append(jnp.where(lane == (pxy[1, i] + side * (PC - 1)) // 64, 1.0, 0.0))
+    spots = jnp.concatenate(spots, axis=0)
+    sums = []
+    for h_ in range(2):
+        v = rs[pl.ds(h_, 128, stride=8), :]
+        sums.append(jnp.broadcast_to(v[:, 88:89], (128, 128)) * spots)
+    b = jnp.concatenate(split3(jnp.concatenate(sums, axis=0)), axis=1)
+    b = jnp.dot(take[...], b, preferred_element_type=F32)
+    turned[...] = (b[:, 0:128] + (b[:, 128:256] + b[:, 256:384])).T
 
     def column(step, _):
         c = wrap(gy + step, NM)
@@ -389,13 +442,26 @@
             got = jnp.dot(take[...], b, preferred_element_type=F32)
             got = got[:, 0:128] + (got[:, 128:256] + got[:, 256:384])
             for r in range(NG):
-                at = pl.multiple_of((r * NM + c) * 16 + 8 * par, 8)
+                at = pl.multiple_of((r * NM + c) * PITCH + 8 * par, 8)
                 so[pl.ds(at, 8), :] = got[8 * r : 8 * r + 8]
+        across = iota((NG, 128), 1) + c * BY - yy
+        mine = jnp.where((across >= 0) & (across < PC), ends, 0.0)
+        out = jnp.zeros((NG, 128), F32)
+        for i in range(NG):
+            line = pxy[0, i] + side * (PC - 1)
+            hit = (rank == line // BX) & (line - (line // 8) * 8 == gy)
+            out = jnp.where(hit, out + jnp.broadcast_to(mine[i : i + 1], (NG, 128)), out)
+        so[pl.ds(c * PITCH + 16, NG, stride=NM * PITCH), :] = out
+        for w in range(2):
+            so[pl.ds(c * PITCH + 17 + w, NG, stride=NM * PITCH), :] = jnp.broadcast_to(
+                turned[pl.ds(2 * c + w, 1), :], (NG, 128)
+            )
 
         for dx, dz in GX_OFFSETS + ((0, 0),):
             a = wrap(x4 + dx, 4) * 4 + wrap(z4 + dz, 4)
             send = remote(
-                so.at[slot(a * NM + c, 16), :], r2.at[slot(gx * NM + gy, 16), :], sems.at[0], sems.at[1], a, c
+                so.at[slot(a * NM + c, PITCH, USED), :], r2.at[slot(gx * NM + gy, PITCH, USED), :],
+                sems.at[0], sems.at[1], a, c,
             )
             if (dx, dz) == (0, 0):
                 pl.when(step > 0)(send.start)
@@ -408,10 +474,10 @@
 
 def main_kernel(
     off, pg, cp, base_h, old_h, fine_h, fold_h,
-    tend_h, fout_h, norm_h, r2,
-    pxy, base, old, fine, fold, tend, trans, s1, hr, hc, fh, r1, hrn, hcn, fhn, gs, tb, gr, tr, br, hz,
-    pad, hrow, res, mm, cells, ss, rs, so, rolled, take, nv, fout,
-    la, sa, sb, sc, sd, se, lb,
+    tend_h, d0_h, d1_h, fout_h, norm_h, r2,
+    pxy, base, old, fine, fold, tend, d0, d1, ring, trans, s1, hr, hc, fh, r1, hrn, hcn, fhn, gs, tb, gr, tr, br, hz,
+    pad, hrow, res, mm, qs, cells, ss, rs, so, rolled, take, turned, nv, nr, fout,
+    la, sa, sb, sc, sd, se, sf, lb, known,
 ):
     gx = lax.axis_index("gx")
     gy = lax.axis_index("gy")
@@ -419,6 +485,7 @@
     ga = gx_peers(gx)
     gb = gy_peers(gy)
     peers = all_peers(gx, gy)
+    n = NG * NM - 1
     loads = [
         pltpu.make_async_copy(base_h, base, la.at[0]),
         pltpu.make_async_copy(fine_h.at[:, :, 0, :], fine, la.at[1]),
@@ -443,29 +510,56 @@
     own = pltpu.make_async_copy(s1.at[gx], r1.at[gx], lb.at[0])
     own.start()
     pl.semaphore_wait(bar, len(ga) + len(gb))
+    for a in ga:
+        pl.semaphore_signal(known, inc=1, device_id=(a, gy), device_id_type=MESH)
 
     up, down = wrap(gx + 1, NG), wrap(gx + NG - 1, NG)
     right, left = wrap(gy + 1, NM), wrap(gy + NM - 1, NM)
     halos = [
+        remote(fh.at[1], fhn.at[0], sb.at[8], sb.at[9], gx, right),
+        remote(fh.at[0], fhn.at[1], sb.at[10], sb.at[11], gx, left),
         remote(hr.at[1], hrn.at[0], sb.at[0], sb.at[1], up, gy),
         remote(hr.at[0], hrn.at[1], sb.at[2], sb.at[3], down, gy),
         remote(hc.at[1], hcn.at[0], sb.at[4], sb.at[5], gx, right),
         remote(hc.at[0], hcn.at[1], sb.at[6], sb.at[7], gx, left),
-        remote(fh.at[1], fhn.at[0], sb.at[8], sb.at[9], gx, right),
-        remote(fh.at[0], fhn.at[1], sb.at[10], sb.at[11], gx, left),
     ]
+    for h in halos:
+        h.start()
     for a in ga:
         remote(s1.at[a], r1.at[gx], sa.at[0], sa.at[1], a, gy).start()
-    for h in halos:
-        h.start()
 
     loads[2].wait()
     acc = fine_interior(cpl, fine, fold, pad, res)
+    halos[0].wait()
+    halos[1].wait()
+    hrow[0] = fhn[0] * jnp.where(gy > 0, 1.0, 0.0)
+    hrow[1] = fhn[1] * jnp.where(gy < NM - 1, 1.0, 0.0)
+    acc = acc + fine_rows(hrow, fh, res)
+    x = pxy[0, gx]
+    y = pxy[1, gx]
+    restrict(x, gy, fine, fh, qs, res, mm, cells, ss)
+    rs[slot(me, 8), :] = ss[slot(me, 8), :]
+    pl.semaphore_wait(known, len(ga))
+    for a, b in peers:
+        remote(ss.at[slot(a * NM + b, 8, 5), :], rs.at[slot(me, 8, 5), :], sd.at[0], sd.at[1], a, b).start()
+
+    for h in halos[2:]:
+        h.wait()
+    loads[3].wait()
+    bsum = base_tendency(gx, gy, pxy, cpl, base, old, hrn, hcn, hz, ring, tend, d0, d1)
+    puts = [
+        pltpu.make_async_copy(tend, tend_h, lb.at[3]),
+        pltpu.make_async_copy(d0, d0_h, lb.at[4]),
+        pltpu.make_async_copy(d1, d1_h, lb.at[5]),
+        pltpu.make_async_copy(fout, fout_h, lb.at[6]),
+        pltpu.make_async_copy(so.at[slot(me, PITCH), :], r2.at[slot(me, PITCH), :], lb.at[7]),
+        pltpu.make_async_copy(nv, norm_h, lb.at[8]),
+    ]
+    for k in range(3):
+        puts[k].start()
 
     own.wait()
     wait_bytes(r1.at[pl.ds(0, NG - 1)], sa.at[1])
-    x = pxy[0, gx]
-    y = pxy[1, gx]
     tb[0] = r1[jnp.maximum(x - 1, 0) // BX, 0:32, :]
     tb[1] = r1[(x + PC) // BX, 0:32, :]
     for j in range(NM):
@@ -490,17 +584,13 @@
         def _():
             near.start()
 
-    for h in halos:
-        h.wait()
-    loads[3].wait()
-    hrow[0] = fhn[0]
-    hrow[1] = fhn[1]
-    bsum = base_tendency(gx, gy, pxy, cpl, base, old, hrn, hcn, hz, tend)
-    tput = pltpu.make_async_copy(tend, tend_h, lb.at[3])
-    tput.start()
+    wait_bytes(rs.at[pl.ds(0, 5 * n), :], sd.at[1])
+    compose_send(gx, gy, pxy, rs, so, rolled, take, turned, r2, se)
+    puts[4].start()
 
     mine.wait()
     wait_bytes(gr.at[pl.ds(0, NM - 1)], sc.at[1])
+    hrow[...] = jnp.zeros((2, 32, 384), F32)
     for ref, target, k in ends:
         far = remote(tb.at[k], ref.at[gy], sc.at[2 + 2 * k], sc.at[3 + 2 * k], gx, target)
         near = pltpu.make_async_copy(tb.at[k], ref.at[gy], lb.at[2])
@@ -516,12 +606,13 @@
             hrow[k] = edge_row(y, ref)
 
     cols = edge_columns(x, y, gy, gr)
-    acc = acc + fine_edges(cols, hrow, fh, fine, res)
+    acc = acc + fine_rows(hrow, fh, res)
+    acc = acc + fine_columns(cols, fine, res)
     norm = jnp.sum(bsum + acc * (1.0 / 9.0), axis=(0, 1), keepdims=True)
-    restrict(x, gy, norm, res, mm, cells, ss)
-    rs[slot(me, 8), :] = ss[slot(me, 8), :]
+    nv[...] = jnp.broadcast_to(norm, (8, 128))
+    nr[slot(me, 8), :] = jnp.broadcast_to(norm, (8, 128))
     for a, b in peers:
-        remote(ss.at[slot(a * NM + b, 8, 4), :], rs.at[slot(me, 8, 4), :], sd.at[0], sd.at[1], a, b).start()
+        remote(nv.at[pl.ds(0, 1), :], nr.at[slot(me, 8, 1), :], sf.at[0], sf.at[1], a, b).start()
 
     def write(p, _):
         for t in range(2):
@@ -530,27 +621,19 @@
         return 0
 
     lax.fori_loop(0, 32, write, 0)
-    fput = pltpu.make_async_copy(fout, fout_h, lb.at[4])
-    fput.start()
-
-    n = NG * NM - 1
-    wait_bytes(rs.at[pl.ds(0, 4 * n), :], sd.at[1])
-    compose_send(gx, gy, pxy, rs, so, rolled, take, r2, se)
-    keep = pltpu.make_async_copy(so.at[slot(me, 16), :], r2.at[slot(me, 16), :], lb.at[5])
-    keep.start()
-    total = jnp.sum(rs[pl.ds(0, 128, stride=8), :], axis=0, keepdims=True)
-    nv[...] = jnp.broadcast_to(jnp.sqrt(total[:, 127:128]), (8, 128))
-    nput = pltpu.make_async_copy(nv, norm_h, lb.at[6])
-    nput.start()
-    nput.wait()
-    keep.wait()
-    tput.wait()
-    fput.wait()
+    puts[3].start()
+    wait_bytes(nr.at[pl.ds(0, n), :], sf.at[1])
+    wait_bytes(nr.at[pl.ds(0, n), :], sf.at[0])
+    total = jnp.sum(nr[pl.ds(0, 128, stride=8), :], axis=0, keepdims=True)
+    nv[...] = jnp.broadcast_to(jnp.sqrt(total), (8, 128))
+    puts[5].start()
+    for put in puts:
+        put.wait()
     wait_bytes(r1.at[pl.ds(0, NG - 1)], sa.at[0])
     wait_bytes(gr.at[pl.ds(0, NM - 1)], sc.at[0])
-    wait_bytes(rs.at[pl.ds(0, 4 * n), :], sd.at[0])
-    wait_bytes(so.at[pl.ds(0, 16 * n), :], se.at[0])
-    wait_bytes(so.at[pl.ds(0, 16 * n), :], se.at[1])
+    wait_bytes(rs.at[pl.ds(0, 5 * n), :], sd.at[0])
+    wait_bytes(so.at[pl.ds(0, USED * n), :], se.at[0])
+    wait_bytes(so.at[pl.ds(0, USED * n), :], se.at[1])
 
 
 def main(off, pg, cp, base, old, fine, fold):
@@ -558,9 +641,9 @@
     dma = pltpu.SemaphoreType.DMA
     return pl.pallas_call(
         main_kernel,
-        out_shape=(shape(32, BX, BY), shape(32, FR, FC), shape(8, 128), shape(2048, 128)),
+        out_shape=(shape(32, BX, BY),) * 3 + (shape(32, FR, FC), shape(8, 128), shape(NG * NM * PITCH, 128)),
         in_specs=[sspec()] * 3 + [hbm] * 4,
-        out_specs=(hbm,) * 4,
+        out_specs=(hbm,) * 6,
         scratch_shapes=[
             pltpu.SMEM((2, NG), jnp.int32),
             VM((32, BX, BY), F32),
@@ -568,6 +651,9 @@
             VM((32, FR, FC), F32),
             VM((32, FR, FC), F32),
             VM((32, BX, BY), F32),
+            VM((32, BX, BY), F32),
+            VM((32, BX, BY), F32),
+            VM((4, BX, BY), F32),
             VM((128, 16, 128), F32),
             VM((NG, 64, 128), F32),
             VM((2, 32, 128), F32),
@@ -587,13 +673,16 @@
             VM((2, 32, 384), F32),
             VM((3 * 32 * 40, 128), F32),
             VM((3, 32, 16, 128), F32),
+            VM((16 * 40, 128), F32),
             VM((32, 16, 128), F32),
             VM((1024, 128), F32),
             VM((1024, 128), F32),
-            VM((2048, 128), F32),
+            VM((NG * NM * PITCH, 128), F32),
             VM((4, 128, 128), F32),
             VM((128, 256), jnp.bfloat16),
+            VM((128, 128), F32),
             VM((8, 128), F32),
+            VM((1024, 128), F32),
             VM((32, FR, FC), F32),
             dma((4,)),
             dma((2,)),
@@ -601,7 +690,9 @@
             dma((6,)),
             dma((2,)),
             dma((2,)),
-            dma((7,)),
+            dma((2,)),
+            dma((9,)),
+            pltpu.SemaphoreType.REGULAR,
         ],
         compiler_params=pltpu.CompilerParams(collective_id=0, has_side_effects=True),
     )(off, pg, cp, base, old, fine, fold)
@@ -610,74 +701,98 @@
 PARTS = 4
 
 
-def merge_kernel(off, tend, ri, fout, nv, out, fres, norm, covered, fine, sem):
-    step = pl.program_id(0)
+def merge_kernel(off, tend_h, d0_h, d1_h, r2, fout, nv, out_h, fres, norm, tend, d0, d1, ri, fine, sem):
+    r = lax.axis_index("gx")
+    c = lax.axis_index("gy")
+    slots = [pl.ds(128 // PARTS * k, 128 // PARTS) for k in range(PARTS)]
+    levels = 8 // PARTS
+
+    def copies(pairs, at):
+        return [[pltpu.make_async_copy(a, b, sem.at[at + k]) for a, b in pairs(k)] for k in range(PARTS)]
+
+    def planes(k):
+        return [pl.ds(8 * f + levels * k, levels) for f in range(4)]
+
     piece = 32 // PARTS
-    ins = [
-        pltpu.make_async_copy(fout.at[pl.ds(piece * k, piece)], fine.at[pl.ds(piece * k, piece)], sem.at[k])
+    here = [pl.ds(piece * k, piece) for k in range(PARTS)]
+    got = [pltpu.make_async_copy(r2, ri, sem.at[0])]
+    had = [
+        [pltpu.make_async_copy(a.at[s], b.at[s], sem.at[1 + k]) for a, b in ((tend_h, tend), (d0_h, d0), (d1_h, d1)) for s in planes(k)]
         for k in range(PARTS)
     ]
-    outs = [
-        pltpu.make_async_copy(fine.at[pl.ds(piece * k, piece)], fres.at[pl.ds(piece * k, piece), :, 0, :], sem.at[PARTS + k])
-        for k in range(PARTS)
-    ]
-
-    @pl.when(step == 0)
-    def _():
-        for copy in ins:
+    give = [[pltpu.make_async_copy(tend.at[s], out_h.at[s], sem.at[1 + PARTS + k]) for s in planes(k)] for k in range(PARTS)]
+    take = [pltpu.make_async_copy(fout.at[here[k]], fine.at[here[k]], sem.at[1 + 2 * PARTS + k]) for k in range(PARTS)]
+    put = [pltpu.make_async_copy(fine.at[here[k]], fres.at[here[k], :, 0, :], sem.at[1 + 3 * PARTS + k]) for k in range(PARTS)]
+    got[0].start()
+    for k in range(PARTS):
+        for copy in had[k]:
             copy.start()
-        r = lax.axis_index("gx")
-        c = lax.axis_index("gy")
-        row = iota((BX, BY), 0)
-        lane = iota((BX, BY), 1)
-        inside = jnp.zeros((BX, BY), F32)
-        for g in range(NG):
-            x = off[0, g] - r * BX
-            y = off[1, g] - c * BY
-            inside = jnp.where((row >= x) & (row < x + PC) & (lane >= y) & (lane < y + PC), 1.0, inside)
-        covered[...] = inside
-        norm[...] = nv[0:1, 0:1]
-
-    for t in range(8):
-        inside = covered[8 * t : 8 * t + 8, :] > 0.5
-        for p in range(piece):
-            got = ri[pl.ds((p // 2) * 128 + (p % 2) * 8 + t, 8, stride=16), :]
-            out[p, 8 * t : 8 * t + 8, :] = jnp.where(inside, got, tend[p, 8 * t : 8 * t + 8, :])
-
     for k in range(PARTS):
-
-        @pl.when(step == k)
-        def _():
-            ins[k].wait()
-            outs[k].start()
-
-    @pl.when(step == PARTS - 1)
-    def _():
-        for copy in outs:
+        take[k].start()
+    row = iota((8, BY), 0)
+    lane = iota((8, BY), 1)
+    last = [jnp.zeros((8, BY), F32) for t in range(8)]
+    east = [jnp.zeros((8, BY), F32) for t in range(8)]
+    for g in range(NG):
+        x = off[0, g] - r * BX
+        y = off[1, g] - c * BY
+        across = (lane >= y) & (lane < y + PC)
+        edge = lane == y + PC - 1
+        for t in range(8):
+            last[t] = jnp.where((row + 8 * t == x + PC - 1) & across, 1.0, last[t])
+            east[t] = jnp.where((row + 8 * t >= x) & (row + 8 * t < x + PC) & edge, 1.0, east[t])
+    norm[...] = nv[0:1, 0:1]
+    flat = ri.reshape(128 * PITCH, 128)
+    got[0].wait()
+    for k in range(PARTS):
+        for copy in had[k]:
             copy.wait()
-
-
-def merge(off, tend, ri, fout, nv):
+        for l in range(levels * k, levels * k + levels):
+            ends = []
+            turn = []
+            for side in range(2):
+                at = (2 * l + side) * 8 * PITCH + 16
+                ends.append(flat[pl.ds(at, 8, stride=PITCH), :])
+                turn.append([pltpu.roll(flat[pl.ds(at + 1 + w, 8, stride=PITCH), :], 128 - 8 * r, 1) for w in range(2)])
+            for t in range(8):
+                tile = slice(8 * t, 8 * t + 8)
+                e0 = jnp.where(last[t] > 0.5, ends[1], ends[0])
+                e1 = [
+                    jnp.where(lane < 64, *[jnp.broadcast_to(turn[side][w][:, t : t + 1], (8, 128)) for w in range(2)])
+                    for side in range(2)
+                ]
+                e1 = jnp.where(east[t] > 0.5, e1[1], e1[0])
+                for f in range(4):
+                    p = 8 * f + l
+                    new = flat[pl.ds((p // 2) * 8 * PITCH + (p % 2) * 8 + t, 8, stride=PITCH), :]
+                    edge = e0 * d0[p, tile, :] + e1 * d1[p, tile, :]
+                    tend[p, tile, :] = tend[p, tile, :] + new + (0.15 / 9) * edge
+        for copy in give[k]:
+            copy.start()
+        take[k].wait()
+        put[k].start()
+    for k in range(PARTS):
+        for copy in give[k]:
+            copy.wait()
+        put[k].wait()
+
+
+def merge(off, tend, d0, d1, ri, fout, nv):
     hbm = pl.BlockSpec(memory_space=pl.ANY)
-    piece = 32 // PARTS
     return pl.pallas_call(
         merge_kernel,
-        grid=(PARTS,),
         out_shape=(shape(32, BX, BY), shape(32, FR, 1, FC), shape(1, 1)),
-        in_specs=[
-            sspec(),
-            pl.BlockSpec((piece, BX, BY), lambda i: (i, 0, 0)),
-            pl.BlockSpec((piece * 64, 128), lambda i: (i, 0)),
-            hbm,
-            pl.BlockSpec((8, 128), lambda i: (0, 0)),
+        in_specs=[sspec()] + [hbm] * 5 + [vspec()],
+        out_specs=(hbm, hbm, vspec()),
+        scratch_shapes=[
+            VM((32, BX, BY), F32),
+            VM((32, BX, BY), F32),
+            VM((32, BX, BY), F32),
+            VM((NG * NM, PITCH, 128), F32),
+            VM((32, FR, FC), F32),
+            pltpu.SemaphoreType.DMA((1 + 4 * PARTS,)),
         ],
-        out_specs=(
-            pl.BlockSpec((piece, BX, BY), lambda i: (i, 0, 0)),
-            hbm,
-            pl.BlockSpec((1, 1), lambda i: (0, 0)),
-        ),
-        scratch_shapes=[VM((BX, BY), F32), VM((32, FR, FC), F32), pltpu.SemaphoreType.DMA((2 * PARTS,))],
-    )(off, tend, ri, fout, nv)
+    )(off, tend, d0, d1, ri.reshape(NG * NM, PITCH, 128), fout, nv)
 
 
 def local(base_state, base_old, fine_state, fine_old, coupling, patch_offsets, patch_group):
@@ -686,8 +801,8 @@
     fine = fine_state.reshape(32, FR, 1, FC)
     fold = fine_old.reshape(32, FR, 1, FC)
     off = patch_offsets.T
-    tend, fout, nv, r2 = main(off, patch_group, coupling, base, old, fine, fold)
-    bout, fres, norm = merge(off, tend, r2, fout, nv)
+    tend, d0, d1, fout, nv, r2 = main(off, patch_group, coupling, base, old, fine, fold)
+    bout, fres, norm = merge(off, tend, d0, d1, r2, fout, nv)
     return (
         bout.reshape(4, 8, BX, BY),
         fres.reshape(4, 8, 1, FR, FC),

time: 54.9 us -> 50.1 us (0.913)
  Pallas kernels: 54 us -> 49.3 us
    pallas_call x2, Pallas kernels: 54 us -> 49.3 us  [the longest x1 44 us: main(): pl.pallas_call(main_kernel, out_shape=(shape(32, BX, BY),) * 3 + (shape(3...]
where the time goes in v4:
time: 50.1 us; the launch traced here: 50 us
  Pallas kernels  49.3 us (98%)
  between operations  0.64 us (1%)
    pallas_call x1, Pallas kernels, main(): pl.pallas_call(main_kernel, out_shape=(shape(32, BX, BY),) * 3 + (shape(3...  44 us
    pallas_call x1, Pallas kernels, merge(): pl.pallas_call(merge_kernel, out_shape=(shape(32, BX, BY), shape(32, FR,...  5.39 us

profile of v4, /device:TPU:1, one launch (start us, length us, event | category | flops | bytes accessed | tf_op | source)
XLA Modules:
  0.0 50.0 jit_solution(9827485220561359247)
XLA Ops:
  0.6 44.0 %shard_map.94 = (f32[32,64,128]{2,1,0:T(8,128)}, f32[32,64,128]{2,1,0:T(8,128)}, f32[32,64,128]{2,1,0:T(8,128)}, f32[32,33,264]{2,1,0:T(8,128)}, f32[8,128]{1,0:T(8,128)}, /*index=5*/f32[3072,128]{1,0:T(8,128)}) custom-call(s32[2,16]{1,0:T(2,128)} %bitcast.14, s32[16]{0:T(128)} %pg.1, f32[4,4]{1,0:T(4,128)} %cp.1, f32[32,64,128]{2,1,0:T(8,128)} %bitcast.12, ...), custom_call_target="tpu_custom_call" | custom-call | tf_op jit(solution)/shard_map/pallas_call | solution.py:642
  44.6 5.4 %shard_map.95 = (f32[32,64,128]{2,1,0:T(8,128)}, f32[32,33,1,264]{3,2,1,0:T(1,128)}, f32[1,1]{1,0:T(1,128)}) custom-call(s32[2,16]{1,0:T(2,128)} %bitcast.15, f32[32,64,128]{2,1,0:T(8,128)} %get-tuple-element.12.tend_h, f32[32,64,128]{2,1,0:T(8,128)} %get-tuple-element.13.d0_h, f32[32,64,128]{2,1,0:T(8,128)} %get-tuple-element.14.d1_h, ...), custom_call_target="tpu_custom_call" | custom-call | tf_op jit(solution)/shard_map/pallas_call | solution.py:782

commit v5 on v4

--- a/solution.py
+++ b/solution.py
@@ -98,7 +98,9 @@
 
 
 PITCH = 24
-USED = 19
+USED = 18
+EARLY = 0
+HALF = 4
 KB = 0.02
 KF = 0.02 * 9
 
@@ -206,7 +208,7 @@
     return cells
 
 
-def fine_interior(cpl, fine, old, pad, res):
+def fine_fill(fine, pad):
     for f in range(4):
         pad[f * 10] = jnp.zeros((56, 384), F32)
         pad[f * 10 + 9] = jnp.zeros((56, 384), F32)
@@ -220,6 +222,9 @@
         return 0
 
     lax.fori_loop(0, 32, fill, 0)
+
+
+def fine_levels(first, stop, acc, cpl, old, pad, res):
     own = 1.0 + 4 * KF + 0.1
 
     def level(l, acc):
@@ -252,7 +257,7 @@
                     acc = acc + sq
         return acc
 
-    return lax.fori_loop(0, 8, level, jnp.zeros((8, 128), F32))
+    return lax.fori_loop(first, stop, level, acc)
 
 
 def edge_columns(x, y, j, gr):
@@ -381,7 +386,7 @@
     return hi, mid, (rest - mid.astype(F32)).astype(jnp.bfloat16)
 
 
-def compose_send(gx, gy, pxy, rs, so, rolled, take, turned, r2, sems):
+def compose_rows(gy, pxy, take):
     n = iota((1, 256), 1)
     h = n // 128
     g = (n - h * 128) // 8
@@ -394,6 +399,9 @@
     row = away - (away // 8) * 8 + 8 * h
     octet = jnp.where(row <= 10, (start + row - gy) // 8, -1)
     take[...] = jnp.where(iota((128, 256), 0) == octet, 1.0, 0.0).astype(jnp.bfloat16)
+
+
+def compose_prepare(gx, pxy, rs, rolled, take, turned, lines):
     for i in range(NG):
         v = [rs[pl.ds(i * 64 + q, 8, stride=8), :] for q in range(4)]
         shift = jnp.broadcast_to(lax.rem(pxy[1, i], BY), (8, 128))
@@ -403,8 +411,6 @@
         for q in range(4):
             rolled[q, 8 * i : 8 * i + 8, :] = v[q]
     lane = iota((8, 128), 1)
-    x4 = gx // 4
-    z4 = gx - 4 * x4
     side = gx - 2 * (gx // 2)
     rank = iota((NG, 128), 0)
     yy = jnp.zeros((NG, 128), jnp.int32)
@@ -415,6 +421,7 @@
     for bit in range(7):
         shift, odd = shift // 2, shift - 2 * (shift // 2) == 1
         ends = jnp.where(odd, pltpu.roll(ends, 1 << bit, 1), ends)
+    lines[...] = ends
     spots = []
     for i in range(NG):
         spots.append(jnp.where(lane == (pxy[1, i] + side * (PC - 1)) // 64, 1.0, 0.0))
@@ -427,6 +434,17 @@
     b = jnp.dot(take[...], b, preferred_element_type=F32)
     turned[...] = (b[:, 0:128] + (b[:, 128:256] + b[:, 256:384])).T
 
+
+def compose_send(first, stop, gx, gy, pxy, so, rolled, take, turned, lines, r2, sems):
+    lane = iota((8, 128), 1)
+    side = gx - 2 * (gx // 2)
+    rank = iota((NG, 128), 0)
+    yy = jnp.zeros((NG, 128), jnp.int32)
+    for i in range(NG):
+        yy = jnp.where(rank == i, pxy[1, i], yy)
+    ends = lines[...]
+    x4 = gx // 4
+    z4 = gx - 4 * x4
     def column(step, _):
         c = wrap(gy + step, NM)
         inside = []
@@ -452,10 +470,10 @@
             hit = (rank == line // BX) & (line - (line // 8) * 8 == gy)
             out = jnp.where(hit, out + jnp.broadcast_to(mine[i : i + 1], (NG, 128)), out)
         so[pl.ds(c * PITCH + 16, NG, stride=NM * PITCH), :] = out
-        for w in range(2):
-            so[pl.ds(c * PITCH + 17 + w, NG, stride=NM * PITCH), :] = jnp.broadcast_to(
-                turned[pl.ds(2 * c + w, 1), :], (NG, 128)
-            )
+        octet = iota((NG, 128), 1) // 8
+        low = jnp.broadcast_to(turned[pl.ds(2 * c, 1), :], (NG, 128))
+        high = jnp.broadcast_to(pltpu.roll(turned[pl.ds(2 * c + 1, 1), :], 64, 1), (NG, 128))
+        so[pl.ds(c * PITCH + 17, NG, stride=NM * PITCH), :] = jnp.where(octet == rank, low, high)
 
         for dx, dz in GX_OFFSETS + ((0, 0),):
             a = wrap(x4 + dx, 4) * 4 + wrap(z4 + dz, 4)
@@ -469,14 +487,14 @@
                 send.start()
         return 0
 
-    lax.fori_loop(0, NM, column, 0)
+    lax.fori_loop(first, stop, column, 0)
 
 
 def main_kernel(
     off, pg, cp, base_h, old_h, fine_h, fold_h,
     tend_h, d0_h, d1_h, fout_h, norm_h, r2,
     pxy, base, old, fine, fold, tend, d0, d1, ring, trans, s1, hr, hc, fh, r1, hrn, hcn, fhn, gs, tb, gr, tr, br, hz,
-    pad, hrow, res, mm, qs, cells, ss, rs, so, rolled, take, turned, nv, nr, fout,
+    pad, hrow, res, mm, qs, cells, ss, rs, so, rolled, take, turned, lines, nv, nr, fout,
     la, sa, sb, sc, sd, se, sf, lb, known,
 ):
     gx = lax.axis_index("gx")
@@ -509,6 +527,9 @@
     fh[1] = jnp.concatenate([fine[:, FR - 1, :], blank], axis=1)
     own = pltpu.make_async_copy(s1.at[gx], r1.at[gx], lb.at[0])
     own.start()
+    fine_fill(fine, pad)
+    loads[2].wait()
+    acc = fine_levels(0, EARLY, jnp.zeros((8, 128), F32), cpl, fold, pad, res)
     pl.semaphore_wait(bar, len(ga) + len(gb))
     for a in ga:
         pl.semaphore_signal(known, inc=1, device_id=(a, gy), device_id_type=MESH)
@@ -528,8 +549,7 @@
     for a in ga:
         remote(s1.at[a], r1.at[gx], sa.at[0], sa.at[1], a, gy).start()
 
-    loads[2].wait()
-    acc = fine_interior(cpl, fine, fold, pad, res)
+    acc = fine_levels(EARLY, 8, acc, cpl, fold, pad, res)
     halos[0].wait()
     halos[1].wait()
     hrow[0] = fhn[0] * jnp.where(gy > 0, 1.0, 0.0)
@@ -584,8 +604,10 @@
         def _():
             near.start()
 
+    compose_rows(gy, pxy, take)
     wait_bytes(rs.at[pl.ds(0, 5 * n), :], sd.at[1])
-    compose_send(gx, gy, pxy, rs, so, rolled, take, turned, r2, se)
+    compose_prepare(gx, pxy, rs, rolled, take, turned, lines)
+    compose_send(0, HALF, gx, gy, pxy, so, rolled, take, turned, lines, r2, se)
     puts[4].start()
 
     mine.wait()
@@ -613,6 +635,8 @@
     nr[slot(me, 8), :] = jnp.broadcast_to(norm, (8, 128))
     for a, b in peers:
         remote(nv.at[pl.ds(0, 1), :], nr.at[slot(me, 8, 1), :], sf.at[0], sf.at[1], a, b).start()
+
+    compose_send(HALF, NM, gx, gy, pxy, so, rolled, take, turned, lines, r2, se)
 
     def write(p, _):
         for t in range(2):
@@ -681,6 +705,7 @@
             VM((4, 128, 128), F32),
             VM((128, 256), jnp.bfloat16),
             VM((128, 128), F32),
+            VM((NG, 128), F32),
             VM((8, 128), F32),
             VM((1024, 128), F32),
             VM((32, FR, FC), F32),
@@ -715,7 +740,7 @@
 
     piece = 32 // PARTS
     here = [pl.ds(piece * k, piece) for k in range(PARTS)]
-    got = [pltpu.make_async_copy(r2, ri, sem.at[0])]
+    got = [pltpu.make_async_copy(r2.at[:, 0:USED, :], ri.at[:, 0:USED, :], sem.at[0])]
     had = [
         [pltpu.make_async_copy(a.at[s], b.at[s], sem.at[1 + k]) for a, b in ((tend_h, tend), (d0_h, d0), (d1_h, d1)) for s in planes(k)]
         for k in range(PARTS)
@@ -753,7 +778,8 @@
             for side in range(2):
                 at = (2 * l + side) * 8 * PITCH + 16
                 ends.append(flat[pl.ds(at, 8, stride=PITCH), :])
-                turn.append([pltpu.roll(flat[pl.ds(at + 1 + w, 8, stride=PITCH), :], 128 - 8 * r, 1) for w in range(2)])
+                row17 = flat[pl.ds(at + 1, 8, stride=PITCH), :]
+                turn.append([pltpu.roll(row17, lax.rem(256 - 8 * r - 64 * w, 128), 1) for w in range(2)])
             for t in range(8):
                 tile = slice(8 * t, 8 * t + 8)
                 e0 = jnp.where(last[t] > 0.5, ends[1], ends[0])

time: 50.1 us -> 48.8 us (0.974)
  Pallas kernels: 49.3 us -> 47.9 us
    pallas_call x1, Pallas kernels: 44 us -> 42.7 us  [main(): pl.pallas_call(main_kernel, out_shape=(shape(32, BX, BY),) * 3 + (shape(3...]
where the time goes in v5:
time: 48.8 us; the launch traced here: 48.6 us
  Pallas kernels  47.9 us (98%)
  between operations  0.64 us (1%)
    pallas_call x1, Pallas kernels, main(): pl.pallas_call(main_kernel, out_shape=(shape(32, BX, BY),) * 3 + (shape(3...  42.7 us
    pallas_call x1, Pallas kernels, merge(): pl.pallas_call(merge_kernel, out_shape=(shape(32, BX, BY), shape(32, FR,...  5.28 us

profile of v5, /device:TPU:1, one launch (start us, length us, event | category | flops | bytes accessed | tf_op | source)
XLA Modules:
  0.0 48.6 jit_solution(15575738013243656215)
XLA Ops:
  0.6 42.7 %shard_map.94 = (f32[32,64,128]{2,1,0:T(8,128)}, f32[32,64,128]{2,1,0:T(8,128)}, f32[32,64,128]{2,1,0:T(8,128)}, f32[32,33,264]{2,1,0:T(8,128)}, f32[8,128]{1,0:T(8,128)}, /*index=5*/f32[3072,128]{1,0:T(8,128)}) custom-call(s32[2,16]{1,0:T(2,128)} %bitcast.14, s32[16]{0:T(128)} %pg.1, f32[4,4]{1,0:T(4,128)} %cp.1, f32[32,64,128]{2,1,0:T(8,128)} %bitcast.12, ...), custom_call_target="tpu_custom_call" | custom-call | tf_op jit(solution)/shard_map/pallas_call | solution.py:666
  43.3 5.3 %shard_map.95 = (f32[32,64,128]{2,1,0:T(8,128)}, f32[32,33,1,264]{3,2,1,0:T(1,128)}, f32[1,1]{1,0:T(1,128)}) custom-call(s32[2,16]{1,0:T(2,128)} %bitcast.15, f32[32,64,128]{2,1,0:T(8,128)} %get-tuple-element.12.tend_h, f32[32,64,128]{2,1,0:T(8,128)} %get-tuple-element.13.d0_h, f32[32,64,128]{2,1,0:T(8,128)} %get-tuple-element.14.d1_h, ...), custom_call_target="tpu_custom_call" | custom-call | tf_op jit(solution)/shard_map/pallas_call | solution.py:808

commit v6 on v5

--- a/solution.py
+++ b/solution.py
@@ -100,7 +100,7 @@
 PITCH = 24
 USED = 18
 EARLY = 0
-HALF = 4
+HALF = 5
 KB = 0.02
 KF = 0.02 * 9
 
@@ -181,7 +181,8 @@
             )
             after = ring[1] * north
             before = ring[0] * south
-            d0[p] = after - before
+            d0[0, p : p + 1, :] = jnp.sum(before, axis=0, keepdims=True)
+            d0[1, p : p + 1, :] = jnp.sum(after, axis=0, keepdims=True)
             both = after + before
             after = ring[3] * east
             before = ring[2] * west
@@ -446,7 +447,9 @@
     x4 = gx // 4
     z4 = gx - 4 * x4
     def column(step, _):
-        c = wrap(gy + step, NM)
+        half = (step + 1) // 2
+        away = 4 + jnp.where(step - 2 * (step // 2) == 0, half, -half)
+        c = wrap(gy + away, NM)
         inside = []
         for i in range(NG):
             at = lane + c * BY - pxy[1, i]
@@ -482,7 +485,7 @@
                 sems.at[0], sems.at[1], a, c,
             )
             if (dx, dz) == (0, 0):
-                pl.when(step > 0)(send.start)
+                pl.when(away > 0)(send.start)
             else:
                 send.start()
         return 0
@@ -608,7 +611,6 @@
     wait_bytes(rs.at[pl.ds(0, 5 * n), :], sd.at[1])
     compose_prepare(gx, pxy, rs, rolled, take, turned, lines)
     compose_send(0, HALF, gx, gy, pxy, so, rolled, take, turned, lines, r2, se)
-    puts[4].start()
 
     mine.wait()
     wait_bytes(gr.at[pl.ds(0, NM - 1)], sc.at[1])
@@ -637,6 +639,7 @@
         remote(nv.at[pl.ds(0, 1), :], nr.at[slot(me, 8, 1), :], sf.at[0], sf.at[1], a, b).start()
 
     compose_send(HALF, NM, gx, gy, pxy, so, rolled, take, turned, lines, r2, se)
+    puts[4].start()
 
     def write(p, _):
         for t in range(2):
@@ -665,7 +668,7 @@
     dma = pltpu.SemaphoreType.DMA
     return pl.pallas_call(
         main_kernel,
-        out_shape=(shape(32, BX, BY),) * 3 + (shape(32, FR, FC), shape(8, 128), shape(NG * NM * PITCH, 128)),
+        out_shape=(shape(32, BX, BY), shape(2, 32, BY), shape(32, BX, BY)) + (shape(32, FR, FC), shape(8, 128), shape(NG * NM * PITCH, 128)),
         in_specs=[sspec()] * 3 + [hbm] * 4,
         out_specs=(hbm,) * 6,
         scratch_shapes=[
@@ -675,7 +678,7 @@
             VM((32, FR, FC), F32),
             VM((32, FR, FC), F32),
             VM((32, BX, BY), F32),
-            VM((32, BX, BY), F32),
+            VM((2, 32, BY), F32),
             VM((32, BX, BY), F32),
             VM((4, BX, BY), F32),
             VM((128, 16, 128), F32),
@@ -726,7 +729,7 @@
 PARTS = 4
 
 
-def merge_kernel(off, tend_h, d0_h, d1_h, r2, fout, nv, out_h, fres, norm, tend, d0, d1, ri, fine, sem):
+def merge_kernel(off, tend_h, d0, d1_h, r2, fout, nv, out_h, fres, norm, tend, d1, ri, fine, sem):
     r = lax.axis_index("gx")
     c = lax.axis_index("gy")
     slots = [pl.ds(128 // PARTS * k, 128 // PARTS) for k in range(PARTS)]
@@ -742,7 +745,7 @@
     here = [pl.ds(piece * k, piece) for k in range(PARTS)]
     got = [pltpu.make_async_copy(r2.at[:, 0:USED, :], ri.at[:, 0:USED, :], sem.at[0])]
     had = [
-        [pltpu.make_async_copy(a.at[s], b.at[s], sem.at[1 + k]) for a, b in ((tend_h, tend), (d0_h, d0), (d1_h, d1)) for s in planes(k)]
+        [pltpu.make_async_copy(a.at[s], b.at[s], sem.at[1 + k]) for a, b in ((tend_h, tend), (d1_h, d1)) for s in planes(k)]
         for k in range(PARTS)
     ]
     give = [[pltpu.make_async_copy(tend.at[s], out_h.at[s], sem.at[1 + PARTS + k]) for s in planes(k)] for k in range(PARTS)]
@@ -756,6 +759,7 @@
         take[k].start()
     row = iota((8, BY), 0)
     lane = iota((8, BY), 1)
+    first = [jnp.zeros((8, BY), F32) for t in range(8)]
     last = [jnp.zeros((8, BY), F32) for t in range(8)]
     east = [jnp.zeros((8, BY), F32) for t in range(8)]
     for g in range(NG):
@@ -764,6 +768,7 @@
         across = (lane >= y) & (lane < y + PC)
         edge = lane == y + PC - 1
         for t in range(8):
+            first[t] = jnp.where((row + 8 * t == x) & across, 1.0, first[t])
             last[t] = jnp.where((row + 8 * t == x + PC - 1) & across, 1.0, last[t])
             east[t] = jnp.where((row + 8 * t >= x) & (row + 8 * t < x + PC) & edge, 1.0, east[t])
     norm[...] = nv[0:1, 0:1]
@@ -782,7 +787,8 @@
                 turn.append([pltpu.roll(row17, lax.rem(256 - 8 * r - 64 * w, 128), 1) for w in range(2)])
             for t in range(8):
                 tile = slice(8 * t, 8 * t + 8)
-                e0 = jnp.where(last[t] > 0.5, ends[1], ends[0])
+                top = first[t] * ends[0]
+                bottom = last[t] * ends[1]
                 e1 = [
                     jnp.where(lane < 64, *[jnp.broadcast_to(turn[side][w][:, t : t + 1], (8, 128)) for w in range(2)])
                     for side in range(2)
@@ -791,7 +797,7 @@
                 for f in range(4):
                     p = 8 * f + l
                     new = flat[pl.ds((p // 2) * 8 * PITCH + (p % 2) * 8 + t, 8, stride=PITCH), :]
-                    edge = e0 * d0[p, tile, :] + e1 * d1[p, tile, :]
+                    edge = bottom * d0[1, p : p + 1, :] - top * d0[0, p : p + 1, :] + e1 * d1[p, tile, :]
                     tend[p, tile, :] = tend[p, tile, :] + new + (0.15 / 9) * edge
         for copy in give[k]:
             copy.start()
@@ -808,10 +814,9 @@
     return pl.pallas_call(
         merge_kernel,
         out_shape=(shape(32, BX, BY), shape(32, FR, 1, FC), shape(1, 1)),
-        in_specs=[sspec()] + [hbm] * 5 + [vspec()],
+        in_specs=[sspec(), hbm, vspec()] + [hbm] * 3 + [vspec()],
         out_specs=(hbm, hbm, vspec()),
         scratch_shapes=[
-            VM((32, BX, BY), F32),
             VM((32, BX, BY), F32),
             VM((32, BX, BY), F32),
             VM((NG * NM, PITCH, 128), F32),

time: 48.8 us -> 48.4 us (level)
  no operation moved by 1% of the time
where the time goes in v6:
time: 48.4 us; the launch traced here: 48.2 us
  Pallas kernels  47.6 us (98%)
  between operations  0.64 us (1%)
    pallas_call x1, Pallas kernels, main(): pl.pallas_call(main_kernel, out_shape=(shape(32, BX, BY), shape(2, 32, BY...  42.5 us
    pallas_call x1, Pallas kernels, merge(): pl.pallas_call(merge_kernel, out_shape=(shape(32, BX, BY), shape(32, FR,...  5.08 us

profile of v6, /device:TPU:1, one launch (start us, length us, event | category | flops | bytes accessed | tf_op | source)
XLA Modules:
  0.0 48.2 jit_solution(15979171123703139201)
XLA Ops:
  0.6 42.5 %shard_map.94 = (f32[32,64,128]{2,1,0:T(8,128)}, f32[2,32,128]{2,1,0:T(8,128)}, f32[32,64,128]{2,1,0:T(8,128)}, f32[32,33,264]{2,1,0:T(8,128)}, f32[8,128]{1,0:T(8,128)}, /*index=5*/f32[3072,128]{1,0:T(8,128)}) custom-call(s32[2,16]{1,0:T(2,128)} %bitcast.14, s32[16]{0:T(128)} %pg.1, f32[4,4]{1,0:T(4,128)} %cp.1, f32[32,64,128]{2,1,0:T(8,128)} %bitcast.12, ...), custom_call_target="tpu_custom_call" | custom-call | tf_op jit(solution)/shard_map/pallas_call | solution.py:669
  43.1 5.1 %shard_map.95 = (f32[32,64,128]{2,1,0:T(8,128)}, f32[32,33,1,264]{3,2,1,0:T(1,128)}, f32[1,1]{1,0:T(1,128)}) custom-call(s32[2,16]{1,0:T(2,128)} %bitcast.15, f32[32,64,128]{2,1,0:T(8,128)} %get-tuple-element.12.tend_h, f32[2,32,128]{2,1,0:T(8,128)} %get-tuple-element.13.d0, f32[32,64,128]{2,1,0:T(8,128)} %get-tuple-element.14.d1_h, ...), custom_call_target="tpu_custom_call" | custom-call | tf_op jit(solution)/shard_map/pallas_call | solution.py:814
